TPU v7x, 32 devices: a whole 2x2x4 slice. The times are simulated.
32 devices in a mesh: seq: 16 (over z, y, core), mp: 2 (over x).
Axes of the slice: x: 2, y: 2, z: 4, core: 2. Of those that a mesh axis runs over, the one named last changes fastest.
Arguments:
- stream: bfloat16 [2048, 8192], P('seq', 'mp'), may hold values from -17 to 17
- norm_gain: float32 [8192], P('mp'), may hold values from 0.5 to 1.5
- short_outer: bfloat16 [2048, 8192], P('seq', 'mp'), may hold values from -4 to 4
- short_inner: bfloat16 [2048, 8192], P('seq', 'mp'), may hold values from -4 to 4
- short_filter: bfloat16 [128, 8192], P(None, 'mp'), may hold values from -0.5 to 0.5
- long_outer: bfloat16 [2048, 8192], P('seq', 'mp'), may hold values from -4 to 4
- long_inner: bfloat16 [2048, 8192], P('seq', 'mp'), may hold values from -4 to 4
- long_decay: float32 [8192], P('mp'), may hold values from 1e-06 to 0.03
- query_heads: bfloat16 [2048, 8192], P('seq', 'mp'), may hold values from -6 to 6
- key_heads: bfloat16 [2048, 8192], P('seq', 'mp'), may hold values from -6 to 6
Outputs:
- long_mixed: bfloat16 [2048, 8192], P('seq', 'mp')
- attended: bfloat16 [2048, 8192], P('seq', 'mp')
All inputs are finite; a program needn't handle non-finite values.
Results may differ from a plain program's by a relative error of at most 0.013.
Values may be sent and summed in bfloat16 or wider, within the bound.
A program may use at most 64 MiB of HBM per device.

v0:
```python
import functools

import jax
import jax.numpy as jnp
import numpy as np
from jax import lax
from jax.experimental import pallas as pl
from jax.experimental.pallas import tpu as pltpu
from jax.sharding import PartitionSpec as P

HEAD_DIM = 128
CHUNKS = 4
PAIR = 2
EARLY = 2
TILE = 256
MESH = pl.DeviceIdType.MESH


def wave(frequency, place, rows):
    shift = jnp.where(frequency >= rows, rows, 0)
    index = lax.rem((2 * lax.rem(frequency, rows) + 1) * place + shift, 4 * rows)
    return jnp.cos(index.astype(jnp.float32) * (np.pi / (2 * rows)))


def dot(a, b):
    return jnp.dot(a, b, preferred_element_type=jnp.float32)


def kernel(
    n,
    mp,
    channels,
    gain_hbm,
    decay_hbm,
    stream_hbm,
    souter_hbm,
    sinner_hbm,
    filt_hbm,
    louter_hbm,
    linner_hbm,
    query_hbm,
    key_hbm,
    mixed,
    attended,
    gain_ref,
    decay_ref,
    stream,
    souter,
    sinner,
    filt,
    louter,
    linner,
    query,
    fwd,
    inv,
    keys,
    values,
    ext,
    power,
    inv_power,
    cum,
    spectrum,
    weights,
    squares,
    squares_in,
    own_state,
    pair_state,
    group_state,
    next_state,
    carry_in,
    states,
    load_sem,
    key_sem,
    sq_send,
    sq_recv,
    k_send,
    k_recv,
    t_send,
    t_recv,
    v_send,
    v_recv,
    p_send,
    p_recv,
    q_send,
    q_recv,
    e_send,
    e_recv,
):
    me = lax.axis_index("seq")
    col = lax.axis_index("mp")
    rows, width = stream.shape
    wide = width // CHUNKS
    tiles = wide // TILE
    heads = wide // HEAD_DIM
    has_next = me < n - 1
    has_prev = me > 0
    groups = n // PAIR
    group = me // PAIR
    leads = lax.rem(me, PAIR) == 0
    follows = lax.rem(me, PAIR) != 0
    own = pl.ds(rows, rows)
    before = pl.ds(0, rows)

    barrier = pltpu.get_barrier_semaphore()

    def greet(target):
        pl.semaphore_signal(barrier, inc=1, device_id={"seq": target}, device_id_type=MESH)

    @pl.when(has_next)
    def _():
        greet(me + 1)

    @pl.when(has_prev)
    def _():
        greet(me - 1)

    @pl.when(leads)
    def _():
        def greet_leader(k, _):
            greet(lax.rem(me + PAIR * k, n))
            return 0

        lax.fori_loop(1, groups, greet_leader, 0)

    for k in range(1, mp):
        pl.semaphore_signal(
            barrier, inc=1, device_id={"mp": lax.rem(col + k, mp)}, device_id_type=MESH
        )

    pairs = [
        (stream_hbm, stream),
        (filt_hbm, filt),
        (sinner_hbm, sinner),
        (souter_hbm, souter),
        (linner_hbm, linner),
        (louter_hbm, louter),
        (query_hbm, query),
        (gain_hbm, gain_ref),
        (decay_hbm, decay_ref),
    ]
    loads = [pltpu.make_async_copy(s, d, load_sem.at[i]) for i, (s, d) in enumerate(pairs)]
    key_loads = [
        pltpu.make_async_copy(
            key_hbm.at[:, pl.ds(c * wide, wide)], keys.at[c, own], key_sem.at[c]
        )
        for c in range(CHUNKS)
    ]
    key_loads[0].start()
    loads[0].start()
    key_loads[1].start()
    for copy in loads[1:]:
        copy.start()
    for copy in key_loads[EARLY:]:
        copy.start()

    def to_next(buffer, c, send, recv):
        return pltpu.make_async_remote_copy(
            src_ref=buffer.at[c, own],
            dst_ref=buffer.at[c, before],
            send_sem=send.at[c],
            recv_sem=recv.at[c],
            device_id={"seq": lax.rem(me + 1, n)},
            device_id_type=MESH,
        )

    k_copies = [to_next(keys, c, k_send, k_recv) for c in range(CHUNKS)]
    t_copies = [to_next(ext, c, t_send, t_recv) for c in range(CHUNKS)]
    v_copies = [to_next(values, c, v_send, v_recv) for c in range(CHUNKS)]

    @pl.when(me == 0)
    def _():
        for c in range(CHUNKS):
            keys[c, :rows, :] = jnp.zeros((rows, wide), keys.dtype)
            values[c, :rows, :] = jnp.zeros((rows, wide), values.dtype)
            ext[c, :rows, :] = jnp.zeros((rows, wide), ext.dtype)

    greeted = has_next.astype(jnp.int32) + has_prev.astype(jnp.int32) + mp - 1
    pl.semaphore_wait(barrier, jnp.where(leads, greeted + groups - 1, greeted))
    for c in range(EARLY):
        key_loads[c].wait()

        @pl.when(has_next)
        def _(c=c):
            k_copies[c].start()

    loads[0].wait()

    def square(i, acc):
        x = stream[:, pl.ds(pl.multiple_of(i * 128, 128), 128)].astype(jnp.float32)
        return acc + x * x

    squares[...] = lax.fori_loop(
        0, width // 128, square, jnp.zeros((rows, 128), jnp.float32), unroll=4
    )
    sq_copies = [
        pltpu.make_async_remote_copy(
            src_ref=squares,
            dst_ref=squares_in.at[k - 1],
            send_sem=sq_send.at[k - 1],
            recv_sem=sq_recv.at[k - 1],
            device_id={"mp": lax.rem(col + k, mp)},
            device_id_type=MESH,
        )
        for k in range(1, mp)
    ]
    for copy in sq_copies:
        copy.start()
    for copy in loads[1:3] + loads[7:]:
        copy.wait()

    full = (2 * rows, 2 * rows)
    fwd[...] = wave(
        lax.broadcasted_iota(jnp.int32, full, 0), lax.broadcasted_iota(jnp.int32, full, 1), rows
    ).astype(jnp.bfloat16)
    half = (rows, 2 * rows)
    inv[...] = (
        wave(
            lax.broadcasted_iota(jnp.int32, half, 1),
            lax.broadcasted_iota(jnp.int32, half, 0) + rows,
            rows,
        )
        / rows
    ).astype(jnp.bfloat16)

    def spectra(i, _):
        cols = pl.ds(pl.multiple_of(i * TILE, TILE), TILE)
        spectrum[:, cols] = dot(fwd[:, :rows], filt[:, cols])
        return 0

    lax.fori_loop(0, width // TILE, spectra, 0)

    total = squares[...]
    for k, copy in enumerate(sq_copies):
        copy.wait_recv()
        total = total + squares_in[k]
    mean_square = jnp.sum(total, axis=1, keepdims=True) / channels
    norm = 1.0 / jnp.sqrt(mean_square + 0.5)

    for c in range(CHUNKS):

        def short(i, _, c=c):
            cols = pl.ds(pl.multiple_of(c * wide + i * TILE, TILE), TILE)
            x = stream[:, cols].astype(jnp.float32) * gain_ref[:, cols] * norm
            ext[c, own, pl.ds(pl.multiple_of(i * TILE, TILE), TILE)] = (
                sinner[:, cols].astype(jnp.float32) * x
            ).astype(jnp.bfloat16)
            return 0

        lax.fori_loop(0, tiles, short, 0)

        @pl.when(has_next)
        def _(c=c):
            t_copies[c].start()

    for copy in key_loads[EARLY:]:
        copy.wait()

    @pl.when(has_next)
    def _():
        for c in range(EARLY, CHUNKS):
            k_copies[c].start()

    step = lax.broadcasted_iota(jnp.int32, (rows, TILE), 0).astype(jnp.float32)

    def powers(i, _):
        cols = pl.ds(pl.multiple_of(i * TILE, TILE), TILE)
        exponent = step * decay_ref[:, cols]
        power[:, cols] = jnp.exp(-exponent)
        inv_power[:, cols] = jnp.exp(exponent)
        return 0

    lax.fori_loop(0, width // TILE, powers, 0)
    for copy in loads[3:7]:
        copy.wait()
    row = lax.broadcasted_iota(jnp.int32, (rows, 2 * rows), 0)
    column = lax.broadcasted_iota(jnp.int32, (rows, 2 * rows), 1)
    lower = (jnp.where(column >= rows, column - rows, column) <= row).astype(
        jnp.float32
    ).astype(jnp.bfloat16)

    def state_copy(c, target):
        return pltpu.make_async_remote_copy(
            src_ref=group_state.at[c],
            dst_ref=states.at[c, group],
            send_sem=e_send.at[c, target],
            recv_sem=e_recv.at[c, group],
            device_id={"seq": lax.rem(target * PAIR, n)},
            device_id_type=MESH,
        )

    p_copies = [
        pltpu.make_async_remote_copy(
            src_ref=own_state.at[c],
            dst_ref=pair_state.at[c],
            send_sem=p_send.at[c],
            recv_sem=p_recv.at[c],
            device_id={"seq": lax.rem(me + n - 1, n)},
            device_id_type=MESH,
        )
        for c in range(CHUNKS)
    ]
    q_copies = [
        pltpu.make_async_remote_copy(
            src_ref=next_state.at[c],
            dst_ref=carry_in.at[c],
            send_sem=q_send.at[c],
            recv_sem=q_recv.at[c],
            device_id={"seq": lax.rem(me + 1, n)},
            device_id_type=MESH,
        )
        for c in range(CHUNKS)
    ]

    for c in range(CHUNKS):

        @pl.when(has_prev)
        def _(c=c):
            t_copies[c].wait_recv()

        def mix(i, _, c=c):
            here = pl.ds(pl.multiple_of(i * TILE, TILE), TILE)
            cols = pl.ds(pl.multiple_of(c * wide + i * TILE, TILE), TILE)
            x = dot(fwd[...], ext[c, :, here])
            x_re, x_im = x[:rows], x[rows:]
            h_re, h_im = spectrum[:rows, cols], spectrum[rows:, cols]
            y = jnp.concatenate(
                [x_re * h_re - x_im * h_im, x_re * h_im + x_im * h_re], axis=0
            ).astype(jnp.bfloat16)
            conv = dot(inv[...], y)
            long_in = (
                linner[:, cols].astype(jnp.float32) * souter[:, cols].astype(jnp.float32) * conv
            ).astype(jnp.bfloat16)
            v = long_in.astype(jnp.float32) * inv_power[:, cols]
            high = v.astype(jnp.bfloat16)
            low = (v - high.astype(jnp.float32)).astype(jnp.bfloat16)
            sums = dot(lower, jnp.concatenate([high, low], axis=0))
            cum[:, cols] = sums
            own_state[c, :, here] = sums[rows - 1 :] * power[rows - 1 :, cols]
            return 0

        lax.fori_loop(0, tiles, mix, 0)

        @pl.when(follows)
        def _(c=c):
            p_copies[c].start()

        @pl.when(leads)
        def _(c=c):
            p_copies[c].wait_recv()
            rate = decay_ref[:, pl.ds(c * wide, wide)]
            group_state[c] = own_state[c] * jnp.exp(-rate * rows) + pair_state[c]

            def send_state(target, _, c=c):
                state_copy(c, target).start()
                return 0

            lax.fori_loop(group + 1, groups, send_state, 0)

    for c in range(CHUNKS):
        chunk = pl.ds(c * wide, wide)
        rate = decay_ref[:, chunk]

        @pl.when(leads)
        def _(c=c, rate=rate):
            over_group = jnp.exp(-rate * (rows * PAIR))

            def arrive(j, state):
                pltpu.make_async_remote_copy(
                    src_ref=group_state.at[c],
                    dst_ref=states.at[c, j],
                    send_sem=e_send.at[c, group],
                    recv_sem=e_recv.at[c, j],
                    device_id={"seq": j * PAIR},
                    device_id_type=MESH,
                ).wait_recv()
                return state * over_group + states[c, j]

            state = lax.fori_loop(0, group, arrive, jnp.zeros((1, wide), jnp.float32))
            next_state[c] = state * jnp.exp(-rate * rows) + own_state[c]
            q_copies[c].start()
            carry_in[c] = state

        @pl.when(follows)
        def _(c=c):
            q_copies[c].wait_recv()

        carried = carry_in[c]
        carried = carried * jnp.exp(-rate)
        z = 2.0 * rate
        scale = jnp.sqrt(jnp.tanh(0.5 * z) * (1.0 + jnp.exp(-z)))
        for i in range(tiles):
            here = pl.ds(i * TILE, TILE)
            cols = pl.ds(c * wide + i * TILE, TILE)
            part = slice(i * TILE, (i + 1) * TILE)
            conv = (cum[:, cols] + carried[:, part]) * power[:, cols]
            out = (
                louter[:, cols].astype(jnp.float32) * (conv * scale[:, part])
            ).astype(jnp.bfloat16)
            values[c, own, here] = out
            mixed[:, cols] = out

        @pl.when(has_next)
        def _(c=c):
            v_copies[c].start()

    valid = (column <= row + rows) & ((column >= rows) | has_prev)
    for c in range(CHUNKS):

        @pl.when(has_prev)
        def _(c=c):
            k_copies[c].wait_recv()

        def score(h, _, c=c):
            here = pl.ds(pl.multiple_of(h * HEAD_DIM, HEAD_DIM), HEAD_DIM)
            cols = pl.ds(pl.multiple_of(c * wide + h * HEAD_DIM, HEAD_DIM), HEAD_DIM)
            s = lax.dot_general(
                query[:, cols],
                keys[c, :, here],
                (((1,), (1,)), ((), ())),
                preferred_element_type=jnp.float32,
            ) * HEAD_DIM ** (-0.5)
            s = jnp.where(valid, s, -1e30)
            e = jnp.exp(s - jnp.max(s, axis=1, keepdims=True))
            e = e * (1.0 / jnp.sum(e, axis=1, keepdims=True))
            weights[c, h] = e.astype(jnp.bfloat16)
            return 0

        lax.fori_loop(0, heads, score, 0, unroll=2)

    for c in range(CHUNKS):

        @pl.when(has_prev)
        def _(c=c):
            v_copies[c].wait_recv()

        def gather(h, _, c=c):
            here = pl.ds(pl.multiple_of(h * HEAD_DIM, HEAD_DIM), HEAD_DIM)
            cols = pl.ds(pl.multiple_of(c * wide + h * HEAD_DIM, HEAD_DIM), HEAD_DIM)
            attended[:, cols] = dot(weights[c, h], values[c, :, here]).astype(jnp.bfloat16)
            return 0

        lax.fori_loop(0, heads, gather, 0, unroll=8)

    for copy in sq_copies:
        copy.wait_send()

    for c in range(CHUNKS):

        @pl.when(follows)
        def _(c=c):
            p_copies[c].wait_send()

        @pl.when(leads)
        def _(c=c):
            q_copies[c].wait_send()

            def sent(target, _):
                state_copy(c, target).wait_send()
                return 0

            lax.fori_loop(group + 1, groups, sent, 0)

    @pl.when(has_next)
    def _():
        for copy in k_copies + t_copies + v_copies:
            copy.wait_send()


def on_device(
    n,
    mp,
    stream,
    norm_gain,
    short_outer,
    short_inner,
    short_filter,
    long_outer,
    long_inner,
    long_decay,
    query_heads,
    key_heads,
):
    rows, width = stream.shape
    wide = width // CHUNKS
    bf16, f32 = jnp.bfloat16, jnp.float32
    anywhere = pl.BlockSpec(memory_space=pltpu.HBM)
    vmem = pl.BlockSpec(memory_space=pltpu.VMEM)
    dma = pltpu.SemaphoreType.DMA
    return pl.pallas_call(
        functools.partial(kernel, n, mp, float(width * mp)),
        out_shape=[jax.ShapeDtypeStruct((rows, width), bf16)] * 2,
        in_specs=[anywhere] * 10,
        out_specs=[vmem] * 2,
        scratch_shapes=[pltpu.VMEM((1, width), f32)] * 2
        + [pltpu.VMEM((rows, width), bf16)] * 7
        + [
            pltpu.VMEM((2 * rows, 2 * rows), bf16),
            pltpu.VMEM((rows, 2 * rows), bf16),
        ]
        + [pltpu.VMEM((CHUNKS, 2 * rows, wide), bf16)] * 3
        + [pltpu.VMEM((rows, width), f32)] * 3
        + [
            pltpu.VMEM((2 * rows, width), f32),
            pltpu.VMEM((CHUNKS, wide // HEAD_DIM, rows, 2 * rows), bf16),
            pltpu.VMEM((rows, 128), f32),
            pltpu.VMEM((mp - 1, rows, 128), f32),
        ]
        + [pltpu.VMEM((CHUNKS, 1, wide), f32)] * 5
        + [
            pltpu.VMEM((CHUNKS, n // PAIR, 1, wide), f32),
            dma((9,)),
            dma((CHUNKS,)),
            dma((mp - 1,)),
            dma((mp - 1,)),
        ]
        + [dma((CHUNKS,))] * 10
        + [dma((CHUNKS, n // PAIR))] * 2,
        compiler_params=pltpu.CompilerParams(
            collective_id=0, has_side_effects=True, vmem_limit_bytes=51 * 1024 * 1024
        ),
    )(
        norm_gain.reshape(1, width),
        long_decay.reshape(1, width),
        stream,
        short_outer,
        short_inner,
        short_filter,
        long_outer,
        long_inner,
        query_heads,
        key_heads,
    )


def solution(mesh):
    return jax.shard_map(
        functools.partial(on_device, mesh.shape["seq"], mesh.shape["mp"]),
        mesh=mesh,
        in_specs=(
            P("seq", "mp"),
            P("mp"),
            P("seq", "mp"),
            P("seq", "mp"),
            P(None, "mp"),
            P("seq", "mp"),
            P("seq", "mp"),
            P("mp"),
            P("seq", "mp"),
            P("seq", "mp"),
        ),
        out_specs=(P("seq", "mp"), P("seq", "mp")),
        check_vma=False,
    )
```

profile of v0, /device:TPU:24, one launch (start us, length us, event | category | flops | bytes accessed | tf_op | source)
XLA Modules:
  0.0 44.8 jit_solution(12049901443920071067)
XLA Ops:
  0.6 0.0 copy-start
  0.6 0.7 %copy-done = f32[4096]{0:T(1024)S(1)} copy-done((f32[4096]{0:T(1024)S(1)}, f32[4096]{0:T(1024)}, u32[]{:S(2)}) %copy-start) | copy-done | bytes 16408
  1.4 0.0 copy-start.1
  1.4 0.7 %copy-done.1 = f32[4096]{0:T(1024)S(1)} copy-done((f32[4096]{0:T(1024)S(1)}, f32[4096]{0:T(1024)}, u32[]{:S(2)}) %copy-start.1) | copy-done | bytes 16408
  2.1 40.8 %shard_map.113 = (bf16[128,4096]{1,0:T(8,128)(2,1)S(1)}, bf16[128,4096]{1,0:T(8,128)(2,1)S(1)}) custom-call(f32[1,4096]{1,0:T(1,128)S(1)} %bitcast.2, f32[1,4096]{1,0:T(1,128)S(1)} %bitcast.3, bf16[128,4096]{1,0:T(8,128)(2,1)} %stream_hbm.1, bf16[128,4096]{1,0:T(8,128)(2,1)} %souter_hbm.1, bf16[128,4096]{1,0:T(8,128)(2,1)} %sinner_hbm.1, ...), custom_call_target="tpu_custom_call" | custom-call | tf_op jit(solution)/shard_map/pallas_call | solution.py:489
  42.9 1.0 %copy.14 = bf16[128,4096]{1,0:T(8,128)(2,1)} copy(bf16[128,4096]{1,0:T(8,128)(2,1)S(1)} %get-tuple-element.4) | data formatting | bytes 2097152
  43.8 1.0 %copy.15 = bf16[128,4096]{1,0:T(8,128)(2,1)} copy(bf16[128,4096]{1,0:T(8,128)(2,1)S(1)} %get-tuple-element.5) | data formatting | bytes 2097152
Async XLA Ops:
  0.6 0.7 %copy-start = (f32[4096]{0:T(1024)S(1)}, f32[4096]{0:T(1024)}, u32[]{:S(2)}) copy-start(f32[4096]{0:T(1024)} %param.11) | copy-start | bytes 49156
  1.4 0.7 %copy-start.1 = (f32[4096]{0:T(1024)S(1)}, f32[4096]{0:T(1024)}, u32[]{:S(2)}) copy-start(f32[4096]{0:T(1024)} %param.17) | copy-start | bytes 49156
where the time goes:
time: 45.6 us; the launch traced here: 44.8 us
  Pallas kernels  40.8 us (89%)
  local copies, waits for them, and re-layouts  3.37 us (7%)
  between operations  0.65 us (1%)
    pallas_call x1, Pallas kernels, on_device(): pl.pallas_call(functools.partial(kernel, n, mp, float(width * mp)), out_s...  40.8 us
    unnamed x6, local copies, waits for them, and re-layouts  3.37 us

commit v1 on v0

--- a/solution.py
+++ b/solution.py
@@ -12,6 +12,7 @@
 CHUNKS = 4
 PAIR = 2
 EARLY = 2
+STORES = 2
 TILE = 256
 MESH = pl.DeviceIdType.MESH
 
@@ -42,15 +43,8 @@
     key_hbm,
     mixed,
     attended,
-    gain_ref,
-    decay_ref,
-    stream,
-    souter,
-    sinner,
-    filt,
-    louter,
-    linner,
-    query,
+    vectors,
+    blocks,
     fwd,
     inv,
     keys,
@@ -86,6 +80,8 @@
     e_send,
     e_recv,
 ):
+    gain_ref, decay_ref = vectors.at[0], vectors.at[1]
+    stream, sinner, filt, souter, linner, louter, query = (blocks.at[i] for i in range(7))
     me = lax.axis_index("seq")
     col = lax.axis_index("mp")
     rows, width = stream.shape
@@ -127,37 +123,28 @@
             barrier, inc=1, device_id={"mp": lax.rem(col + k, mp)}, device_id_type=MESH
         )
 
-    pairs = [
-        (stream_hbm, stream),
-        (filt_hbm, filt),
-        (sinner_hbm, sinner),
-        (souter_hbm, souter),
-        (linner_hbm, linner),
-        (louter_hbm, louter),
-        (query_hbm, query),
-        (gain_hbm, gain_ref),
-        (decay_hbm, decay_ref),
-    ]
-    loads = [pltpu.make_async_copy(s, d, load_sem.at[i]) for i, (s, d) in enumerate(pairs)]
-    key_loads = [
-        pltpu.make_async_copy(
-            key_hbm.at[:, pl.ds(c * wide, wide)], keys.at[c, own], key_sem.at[c]
-        )
-        for c in range(CHUNKS)
-    ]
-    key_loads[0].start()
-    loads[0].start()
-    key_loads[1].start()
-    for copy in loads[1:]:
+    def load(source, target, sem):
+        copy = pltpu.make_async_copy(source, target, sem)
         copy.start()
-    for copy in key_loads[EARLY:]:
-        copy.start()
+
+    def landed(buffer, sem):
+        pltpu.make_async_copy(buffer, buffer, sem).wait()
+
+    def load_key(c, sem):
+        load(key_hbm.at[:, pl.ds(c * wide, wide)], keys.at[c, own], sem)
+
+    for c in range(EARLY):
+        load_key(c, key_sem.at[c])
+    load(stream_hbm, stream, load_sem.at[0])
+    load(sinner_hbm, sinner, load_sem.at[1])
+    load(gain_hbm, gain_ref, load_sem.at[2])
+    load(decay_hbm, decay_ref, load_sem.at[2])
 
     def to_next(buffer, c, send, recv):
         return pltpu.make_async_remote_copy(
             src_ref=buffer.at[c, own],
             dst_ref=buffer.at[c, before],
-            send_sem=send.at[c],
+            send_sem=send.at[0],
             recv_sem=recv.at[c],
             device_id={"seq": lax.rem(me + 1, n)},
             device_id_type=MESH,
@@ -177,21 +164,29 @@
     greeted = has_next.astype(jnp.int32) + has_prev.astype(jnp.int32) + mp - 1
     pl.semaphore_wait(barrier, jnp.where(leads, greeted + groups - 1, greeted))
     for c in range(EARLY):
-        key_loads[c].wait()
+        landed(keys.at[c, own], key_sem.at[c])
 
         @pl.when(has_next)
         def _(c=c):
             k_copies[c].start()
 
-    loads[0].wait()
+    load(filt_hbm, filt, load_sem.at[3])
+    for c in range(EARLY, CHUNKS):
+        load_key(c, key_sem.at[EARLY])
+    load(souter_hbm, souter, load_sem.at[4])
+    load(linner_hbm, linner, load_sem.at[4])
+    load(query_hbm, query, load_sem.at[5])
+    load(louter_hbm, louter, load_sem.at[6])
+    landed(stream, load_sem.at[0])
 
     def square(i, acc):
         x = stream[:, pl.ds(pl.multiple_of(i * 128, 128), 128)].astype(jnp.float32)
         return acc + x * x
 
-    squares[...] = lax.fori_loop(
+    total = lax.fori_loop(
         0, width // 128, square, jnp.zeros((rows, 128), jnp.float32), unroll=4
     )
+    squares[...] = jnp.sum(total.T.reshape(128 // 8, 8, rows), axis=0)
     sq_copies = [
         pltpu.make_async_remote_copy(
             src_ref=squares,
@@ -205,8 +200,38 @@
     ]
     for copy in sq_copies:
         copy.start()
-    for copy in loads[1:3] + loads[7:]:
-        copy.wait()
+    landed(sinner, load_sem.at[1])
+    landed(vectors, load_sem.at[2])
+    total = squares[...]
+    for k, copy in enumerate(sq_copies):
+        copy.wait_recv()
+        total = total + squares_in[k]
+    mean_square = jnp.sum(total, axis=0, keepdims=True) / channels
+    norm = jnp.broadcast_to(1.0 / jnp.sqrt(mean_square + 0.5), (128, rows)).T
+    norm = jnp.concatenate([norm] * (TILE // 128), axis=1)
+
+    for c in range(CHUNKS):
+
+        def short(i, _, c=c):
+            cols = pl.ds(pl.multiple_of(c * wide + i * TILE, TILE), TILE)
+            x = stream[:, cols].astype(jnp.float32) * gain_ref[:, cols] * norm
+            ext[c, own, pl.ds(pl.multiple_of(i * TILE, TILE), TILE)] = (
+                sinner[:, cols].astype(jnp.float32) * x
+            ).astype(jnp.bfloat16)
+            return 0
+
+        lax.fori_loop(0, tiles, short, 0)
+
+        @pl.when(has_next)
+        def _(c=c):
+            t_copies[c].start()
+
+    landed(keys.at[pl.ds(EARLY, CHUNKS - EARLY), own], key_sem.at[EARLY])
+
+    @pl.when(has_next)
+    def _():
+        for c in range(EARLY, CHUNKS):
+            k_copies[c].start()
 
     full = (2 * rows, 2 * rows)
     fwd[...] = wave(
@@ -227,38 +252,8 @@
         spectrum[:, cols] = dot(fwd[:, :rows], filt[:, cols])
         return 0
 
+    landed(filt, load_sem.at[3])
     lax.fori_loop(0, width // TILE, spectra, 0)
-
-    total = squares[...]
-    for k, copy in enumerate(sq_copies):
-        copy.wait_recv()
-        total = total + squares_in[k]
-    mean_square = jnp.sum(total, axis=1, keepdims=True) / channels
-    norm = 1.0 / jnp.sqrt(mean_square + 0.5)
-
-    for c in range(CHUNKS):
-
-        def short(i, _, c=c):
-            cols = pl.ds(pl.multiple_of(c * wide + i * TILE, TILE), TILE)
-            x = stream[:, cols].astype(jnp.float32) * gain_ref[:, cols] * norm
-            ext[c, own, pl.ds(pl.multiple_of(i * TILE, TILE), TILE)] = (
-                sinner[:, cols].astype(jnp.float32) * x
-            ).astype(jnp.bfloat16)
-            return 0
-
-        lax.fori_loop(0, tiles, short, 0)
-
-        @pl.when(has_next)
-        def _(c=c):
-            t_copies[c].start()
-
-    for copy in key_loads[EARLY:]:
-        copy.wait()
-
-    @pl.when(has_next)
-    def _():
-        for c in range(EARLY, CHUNKS):
-            k_copies[c].start()
 
     step = lax.broadcasted_iota(jnp.int32, (rows, TILE), 0).astype(jnp.float32)
 
@@ -270,8 +265,7 @@
         return 0
 
     lax.fori_loop(0, width // TILE, powers, 0)
-    for copy in loads[3:7]:
-        copy.wait()
+    landed(blocks.at[pl.ds(3, 2)], load_sem.at[4])
     row = lax.broadcasted_iota(jnp.int32, (rows, 2 * rows), 0)
     column = lax.broadcasted_iota(jnp.int32, (rows, 2 * rows), 1)
     lower = (jnp.where(column >= rows, column - rows, column) <= row).astype(
@@ -282,7 +276,7 @@
         return pltpu.make_async_remote_copy(
             src_ref=group_state.at[c],
             dst_ref=states.at[c, group],
-            send_sem=e_send.at[c, target],
+            send_sem=e_send.at[target],
             recv_sem=e_recv.at[c, group],
             device_id={"seq": lax.rem(target * PAIR, n)},
             device_id_type=MESH,
@@ -292,7 +286,7 @@
         pltpu.make_async_remote_copy(
             src_ref=own_state.at[c],
             dst_ref=pair_state.at[c],
-            send_sem=p_send.at[c],
+            send_sem=p_send.at[0],
             recv_sem=p_recv.at[c],
             device_id={"seq": lax.rem(me + n - 1, n)},
             device_id_type=MESH,
@@ -303,7 +297,7 @@
         pltpu.make_async_remote_copy(
             src_ref=next_state.at[c],
             dst_ref=carry_in.at[c],
-            send_sem=q_send.at[c],
+            send_sem=q_send.at[0],
             recv_sem=q_recv.at[c],
             device_id={"seq": lax.rem(me + 1, n)},
             device_id_type=MESH,
@@ -356,6 +350,7 @@
 
             lax.fori_loop(group + 1, groups, send_state, 0)
 
+    landed(louter, load_sem.at[6])
     for c in range(CHUNKS):
         chunk = pl.ds(c * wide, wide)
         rate = decay_ref[:, chunk]
@@ -368,7 +363,7 @@
                 pltpu.make_async_remote_copy(
                     src_ref=group_state.at[c],
                     dst_ref=states.at[c, j],
-                    send_sem=e_send.at[c, group],
+                    send_sem=e_send.at[group],
                     recv_sem=e_recv.at[c, j],
                     device_id={"seq": j * PAIR},
                     device_id_type=MESH,
@@ -403,6 +398,7 @@
         def _(c=c):
             v_copies[c].start()
 
+    landed(query, load_sem.at[5])
     valid = (column <= row + rows) & ((column >= rows) | has_prev)
     for c in range(CHUNKS):
 
@@ -444,26 +440,42 @@
     for copy in sq_copies:
         copy.wait_send()
 
-    for c in range(CHUNKS):
-
-        @pl.when(follows)
-        def _(c=c):
-            p_copies[c].wait_send()
-
-        @pl.when(leads)
-        def _(c=c):
-            q_copies[c].wait_send()
-
-            def sent(target, _):
-                state_copy(c, target).wait_send()
-                return 0
-
-            lax.fori_loop(group + 1, groups, sent, 0)
+    def sent(buffer, sem):
+        pltpu.make_async_copy(buffer, buffer, sem).wait()
+
+    @pl.when(follows)
+    def _():
+        sent(own_state, p_send.at[0])
+
+    @pl.when(leads)
+    def _():
+        sent(next_state, q_send.at[0])
+
+        def all_sent(target, _):
+            sent(group_state, e_send.at[target])
+            return 0
+
+        lax.fori_loop(group + 1, groups, all_sent, 0)
 
     @pl.when(has_next)
     def _():
-        for copy in k_copies + t_copies + v_copies:
-            copy.wait_send()
+        sent(keys.at[:, own], k_send.at[0])
+        sent(ext.at[:, own], t_send.at[0])
+        sent(values.at[:, own], v_send.at[0])
+
+
+def store(mixed, attended, mixed_hbm, attended_hbm, sem):
+    rows = mixed.shape[0]
+    parts = [pl.ds(i * rows // STORES, rows // STORES) for i in range(STORES)]
+    copies = [
+        pltpu.make_async_copy(source.at[part], target.at[part], sem.at[k, i])
+        for k, (source, target) in enumerate([(mixed, mixed_hbm), (attended, attended_hbm)])
+        for i, part in enumerate(parts)
+    ]
+    for copy in copies:
+        copy.start()
+    for copy in copies:
+        copy.wait()
 
 
 def on_device(
@@ -486,14 +498,18 @@
     anywhere = pl.BlockSpec(memory_space=pltpu.HBM)
     vmem = pl.BlockSpec(memory_space=pltpu.VMEM)
     dma = pltpu.SemaphoreType.DMA
-    return pl.pallas_call(
+
+    def in_hbm(array):
+        return pltpu.with_memory_space_constraint(array, pltpu.HBM)
+
+    mixed, attended = pl.pallas_call(
         functools.partial(kernel, n, mp, float(width * mp)),
         out_shape=[jax.ShapeDtypeStruct((rows, width), bf16)] * 2,
         in_specs=[anywhere] * 10,
         out_specs=[vmem] * 2,
-        scratch_shapes=[pltpu.VMEM((1, width), f32)] * 2
-        + [pltpu.VMEM((rows, width), bf16)] * 7
-        + [
+        scratch_shapes=[
+            pltpu.VMEM((2, 1, width), f32),
+            pltpu.VMEM((7, rows, width), bf16),
             pltpu.VMEM((2 * rows, 2 * rows), bf16),
             pltpu.VMEM((rows, 2 * rows), bf16),
         ]
@@ -502,25 +518,25 @@
         + [
             pltpu.VMEM((2 * rows, width), f32),
             pltpu.VMEM((CHUNKS, wide // HEAD_DIM, rows, 2 * rows), bf16),
-            pltpu.VMEM((rows, 128), f32),
-            pltpu.VMEM((mp - 1, rows, 128), f32),
+            pltpu.VMEM((8, rows), f32),
+            pltpu.VMEM((mp - 1, 8, rows), f32),
         ]
         + [pltpu.VMEM((CHUNKS, 1, wide), f32)] * 5
         + [
             pltpu.VMEM((CHUNKS, n // PAIR, 1, wide), f32),
-            dma((9,)),
-            dma((CHUNKS,)),
+            dma((7,)),
+            dma((EARLY + 1,)),
             dma((mp - 1,)),
             dma((mp - 1,)),
         ]
-        + [dma((CHUNKS,))] * 10
-        + [dma((CHUNKS, n // PAIR))] * 2,
+        + [dma((1,)), dma((CHUNKS,))] * 5
+        + [dma((n // PAIR,)), dma((CHUNKS, n // PAIR))],
         compiler_params=pltpu.CompilerParams(
             collective_id=0, has_side_effects=True, vmem_limit_bytes=51 * 1024 * 1024
         ),
     )(
-        norm_gain.reshape(1, width),
-        long_decay.reshape(1, width),
+        in_hbm(norm_gain.reshape(1, width)),
+        in_hbm(long_decay.reshape(1, width)),
         stream,
         short_outer,
         short_inner,
@@ -530,6 +546,14 @@
         query_heads,
         key_heads,
     )
+    return pl.pallas_call(
+        store,
+        out_shape=[jax.ShapeDtypeStruct((rows, width), bf16)] * 2,
+        in_specs=[vmem] * 2,
+        out_specs=[anywhere] * 2,
+        scratch_shapes=[dma((2, STORES))],
+        compiler_params=pltpu.CompilerParams(vmem_limit_bytes=1024 * 1024),
+    )(mixed, attended)
 
 
 def solution(mesh):

time: 45.6 us -> 42.2 us (0.925)
  local copies, waits for them, and re-layouts: 3.37 us -> 0 us
    unnamed x6 -> x0, local copies, waits for them, and re-layouts: 3.37 us -> none
    pallas_call x0 -> x1, Pallas kernels: none -> 1.35 us  [on_device(): pl.pallas_call(store, out_shape=[jax.ShapeDtypeStruct((rows, width), bf16...]
    pallas_call x1, Pallas kernels: 40.8 us -> 39.7 us  [on_device(): pl.pallas_call(functools.partial(kernel, n, mp, float(width * mp)), out_s...]
where the time goes in v1:
time: 42.2 us; the launch traced here: 41.7 us
  Pallas kernels  41 us (97%)
  between operations  0.64 us (2%)
    pallas_call x1, Pallas kernels, on_device(): pl.pallas_call(functools.partial(kernel, n, mp, float(width * mp)), out_s...  39.7 us
    pallas_call x1, Pallas kernels, on_device(): pl.pallas_call(store, out_shape=[jax.ShapeDtypeStruct((rows, width), bf16...  1.35 us

profile of v1, /device:TPU:24, one launch (start us, length us, event | category | flops | bytes accessed | tf_op | source)
XLA Modules:
  0.0 41.7 jit_solution(2538171598018284181)
XLA Ops:
  0.6 39.7 %shard_map.113 = (bf16[128,4096]{1,0:T(8,128)(2,1)S(1)}, bf16[128,4096]{1,0:T(8,128)(2,1)S(1)}) custom-call(f32[1,4096]{1,0:T(1,128)} %bitcast.2, f32[1,4096]{1,0:T(1,128)} %bitcast.3, bf16[128,4096]{1,0:T(8,128)(2,1)} %stream_hbm.1, bf16[128,4096]{1,0:T(8,128)(2,1)} %souter_hbm.1, bf16[128,4096]{1,0:T(8,128)(2,1)} %sinner_hbm.1, ...), custom_call_target="tpu_custom_call" | custom-call | tf_op jit(solution)/shard_map/pallas_call | solution.py:505
  40.3 1.3 %shard_map.114 = (bf16[128,4096]{1,0:T(8,128)(2,1)}, bf16[128,4096]{1,0:T(8,128)(2,1)}) custom-call(bf16[128,4096]{1,0:T(8,128)(2,1)S(1)} %get-tuple-element.4.mixed, bf16[128,4096]{1,0:T(8,128)(2,1)S(1)} %get-tuple-element.5.attended), custom_call_target="tpu_custom_call" | custom-call | tf_op jit(solution)/shard_map/pallas_call | solution.py:549

commit v2 on v1

v2 whole, which is shorter than its diff:
```python
import functools

import jax
import jax.numpy as jnp
import numpy as np
from jax import lax
from jax.experimental import pallas as pl
from jax.experimental.pallas import tpu as pltpu
from jax.sharding import PartitionSpec as P

HEAD_DIM = 128
CHUNKS = 4
HALF = CHUNKS // 2
LENT = CHUNKS - 1
GROUP = 4
TILE = 256
STORES = 2
MESH = pl.DeviceIdType.MESH


def wave(frequency, place, rows):
    shift = np.where(frequency >= rows, rows, 0)
    index = ((2 * (frequency % rows) + 1) * place + shift) % (4 * rows)
    return np.cos(index * (np.pi / (2 * rows)))


def waves_of(rows):
    every = np.arange(2 * rows)
    fwd = wave(every[:, None], every[None, :], rows)
    inv = wave(every[None, :], every[:rows, None] + rows, rows) / rows
    return np.concatenate([fwd, inv], axis=0)


def dot(a, b):
    return jnp.dot(a, b, preferred_element_type=jnp.float32)


def dot_nt(a, b):
    return lax.dot_general(a, b, (((1,), (1,)), ((), ())), preferred_element_type=jnp.float32)


def dot_tn(a, b):
    return lax.dot_general(a, b, (((0,), (0,)), ((), ())), preferred_element_type=jnp.float32)


def kernel(
    n,
    mp,
    channels,
    gain_hbm,
    decay_hbm,
    waves_hbm,
    stream_hbm,
    souter_hbm,
    sinner_hbm,
    filt_hbm,
    louter_hbm,
    linner_hbm,
    query_hbm,
    key_hbm,
    mixed,
    attended,
    vectors,
    blocks,
    waves,
    keys,
    values,
    ext,
    relayed,
    next_query,
    lent,
    own_part,
    shares,
    power,
    inv_power,
    cum,
    spectrum,
    weights,
    lent_weights,
    stats,
    stats_in,
    squares,
    squares_in,
    own_state,
    member_state,
    pair_state,
    before_state,
    group_state,
    next_state,
    carry_in,
    states,
    load_sem,
    key_sem,
    sq_send,
    sq_recv,
    k_send,
    k_recv,
    t_send,
    t_recv,
    v_send,
    v_recv,
    r_send,
    r_recv,
    p_send,
    p_recv,
    q_send,
    q_recv,
    g_send,
    g_recv,
    e_send,
    e_recv,
    lend_send,
    lend_recv,
):
    gain_ref, decay_ref = vectors.at[0], vectors.at[1]
    stream, sinner, filt, souter, linner, louter, query = (blocks.at[i] for i in range(7))
    me = lax.axis_index("seq")
    col = lax.axis_index("mp")
    rows, width = stream.shape
    fwd, inv = waves.at[pl.ds(0, 2 * rows)], waves.at[pl.ds(2 * rows, rows)]
    wide = width // CHUNKS
    tiles = wide // TILE
    heads = wide // HEAD_DIM
    has_next = me < n - 1
    has_prev = me > 0
    groups = n // GROUP
    group = me // GROUP
    role = lax.rem(me, GROUP)
    later = groups - 1 - group
    first = role == 0
    lends = role == 1
    borrows = role == 2
    relays = jnp.logical_and(role == 3, later > 0)
    forwards = jnp.logical_and(lends, later > 0)
    even = lax.rem(me, 2) == 0
    own = pl.ds(rows, rows)
    before = pl.ds(0, rows)

    def seq(target):
        return {"seq": lax.rem(target + n, n)}

    barrier = pltpu.get_barrier_semaphore()

    def greet(target, when):
        @pl.when(when)
        def _():
            pl.semaphore_signal(barrier, inc=1, device_id=seq(target), device_id_type=MESH)

    greet(me + 1, has_next)
    greet(me - 1, has_prev)
    greet(me - 2, borrows)
    greet(me + 2, forwards)
    greet(me - 3, jnp.logical_and(first, group > 0))

    @pl.when(even)
    def _():
        def greet_earlier(j, _):
            pl.semaphore_signal(
                barrier, inc=1, device_id=seq(j * GROUP + 2), device_id_type=MESH
            )
            return 0

        lax.fori_loop(0, group, greet_earlier, 0)

    greeted = has_next.astype(jnp.int32) + has_prev.astype(jnp.int32) + mp - 1
    greeted += jnp.where(borrows, 2 * later, 0)
    greeted += (first | relays | forwards).astype(jnp.int32)

    for k in range(1, mp):
        pl.semaphore_signal(
            barrier, inc=1, device_id={"mp": lax.rem(col + k, mp)}, device_id_type=MESH
        )

    def load(source, target, sem):
        pltpu.make_async_copy(source, target, sem).start()

    def landed(buffer, sem):
        pltpu.make_async_copy(buffer, buffer, sem).wait()

    def load_key(c, sem):
        load(key_hbm.at[:, pl.ds(c * wide, wide)], keys.at[c, own], sem)

    others = [c for c in range(1, CHUNKS) if c != HALF]
    last = pl.ds(LENT * wide, wide)
    rest = pl.ds(0, LENT * wide)
    load(query_hbm.at[:, last], query.at[:, last], load_sem.at[6])
    load_key(0, key_sem.at[0])
    load_key(HALF, key_sem.at[1])
    load(stream_hbm, stream, load_sem.at[0])
    load(gain_hbm, gain_ref, load_sem.at[2])
    load(decay_hbm, decay_ref, load_sem.at[2])
    load(waves_hbm, waves, load_sem.at[3])
    load(filt_hbm, filt, load_sem.at[4])
    load(sinner_hbm, sinner, load_sem.at[1])

    def remote(source, target, send, recv, device):
        return pltpu.make_async_remote_copy(
            src_ref=source,
            dst_ref=target,
            send_sem=send,
            recv_sem=recv,
            device_id=device,
            device_id_type=MESH,
        )

    def to_next(buffer, c, send, recv):
        return remote(
            buffer.at[c, own], buffer.at[c, before], send.at[0], recv.at[c], seq(me + 1)
        )

    def to_relay(buffer, c, slot, send):
        return remote(
            buffer.at[c, own], relayed.at[slot], send.at[0], r_recv.at[slot], seq(me - 2)
        )

    k_copies = [to_next(keys, c, k_send, k_recv) for c in range(CHUNKS)]
    t_copies = [to_next(ext, c, t_send, t_recv) for c in range(CHUNKS)]
    v_copies = [to_next(values, c, v_send, v_recv) for c in range(CHUNKS)]
    lent_query = remote(
        query.at[:, last], next_query, lend_send.at[0], lend_recv.at[0], seq(me - 1)
    )
    lent_stats = remote(stats, stats_in, lend_send.at[1], lend_recv.at[1], seq(me + 1))
    lent_values = remote(
        lent, values.at[LENT, before], v_send.at[0], v_recv.at[LENT], seq(me + 1)
    )

    key_relay = [
        later > 1 if c >= HALF else True for c in range(CHUNKS)
    ]
    tail_relay = group == 0
    key_slot = [(c + HALF) % CHUNKS for c in range(CHUNKS)]

    def send_key(c, when=True):
        relay = jnp.logical_and(relays, key_relay[c])
        direct = jnp.logical_and(has_next, jnp.logical_not(relay))
        if c == LENT:
            direct = jnp.logical_and(direct, jnp.logical_not(lends))

        @pl.when(jnp.logical_and(relay, when))
        def _():
            to_relay(keys, c, key_slot[c], k_send).start()

        @pl.when(jnp.logical_and(direct, when))
        def _():
            k_copies[c].start()

    def send_tail(c):
        direct = has_next
        if c >= HALF:
            relay = jnp.logical_and(relays, tail_relay)
            direct = jnp.logical_and(has_next, jnp.logical_not(relay))

            @pl.when(relay)
            def _():
                to_relay(ext, c, CHUNKS + c - HALF, t_send).start()

        @pl.when(direct)
        def _():
            t_copies[c].start()

    def pass_on(buffer, c, slot, recv, when):
        @pl.when(jnp.logical_and(forwards, when))
        def _():
            remote(
                buffer.at[c, own], relayed.at[slot], k_send.at[0], r_recv.at[slot], seq(me + 2)
            ).wait_recv()
            remote(
                relayed.at[slot], buffer.at[c, before], r_send.at[0], recv.at[c], seq(me + 3)
            ).start()

    def pass_key(c):
        pass_on(keys, c, key_slot[c], k_recv, key_relay[c])

    def pass_tail(c):
        pass_on(ext, c, CHUNKS + c - HALF, t_recv, tail_relay)

    def pass_value():
        pass_on(values, 0, CHUNKS + HALF, v_recv, tail_relay)

    @pl.when(me == 0)
    def _():
        for c in range(CHUNKS):
            keys[c, :rows, :] = jnp.zeros((rows, wide), keys.dtype)
            values[c, :rows, :] = jnp.zeros((rows, wide), values.dtype)
            ext[c, :rows, :] = jnp.zeros((rows, wide), ext.dtype)

    pl.semaphore_wait(barrier, greeted)
    origin = group == 0
    late = jnp.logical_and(relays, origin)
    landed(query.at[:, last], load_sem.at[6])

    @pl.when(jnp.logical_and(borrows, jnp.logical_not(origin)))
    def _():
        lent_query.start()

    landed(keys.at[0, own], key_sem.at[0])
    send_key(0, jnp.logical_not(late))
    landed(keys.at[HALF, own], key_sem.at[1])
    for c in others:
        load_key(c, key_sem.at[2 + others.index(c)])
    load(souter_hbm, souter, load_sem.at[5])
    load(linner_hbm, linner, load_sem.at[5])
    load(louter_hbm, louter, load_sem.at[7])
    load(query_hbm.at[:, rest], query.at[:, rest], load_sem.at[8])
    landed(stream, load_sem.at[0])

    def square(i, acc):
        x = stream[:, pl.ds(pl.multiple_of(i * 128, 128), 128)].astype(jnp.float32)
        return acc + x * x

    total = lax.fori_loop(
        0, width // 128, square, jnp.zeros((rows, 128), jnp.float32), unroll=4
    )
    squares[...] = jnp.sum(total.T.reshape(128 // 8, 8, rows), axis=0)
    sq_copies = [
        pltpu.make_async_remote_copy(
            src_ref=squares,
            dst_ref=squares_in.at[k - 1],
            send_sem=sq_send.at[k - 1],
            recv_sem=sq_recv.at[k - 1],
            device_id={"mp": lax.rem(col + k, mp)},
            device_id_type=MESH,
        )
        for k in range(1, mp)
    ]
    for copy in sq_copies:
        copy.start()

    landed(vectors, load_sem.at[2])
    step = lax.broadcasted_iota(jnp.int32, (rows, TILE), 0).astype(jnp.float32)

    def powers(i, _):
        cols = pl.ds(pl.multiple_of(i * TILE, TILE), TILE)
        exponent = step * decay_ref[:, cols]
        power[:, cols] = jnp.exp(-exponent)
        inv_power[:, cols] = jnp.exp(exponent)
        return 0

    lax.fori_loop(0, width // TILE, powers, 0)
    landed(waves, load_sem.at[3])
    landed(filt, load_sem.at[4])

    def spectra(i, _):
        cols = pl.ds(pl.multiple_of(i * TILE, TILE), TILE)
        spectrum[:, cols] = dot(fwd[:, :rows], filt[:, cols])
        return 0

    lax.fori_loop(0, width // TILE // 2, spectra, 0)
    landed(sinner, load_sem.at[1])
    total = squares[...]
    for k, copy in enumerate(sq_copies):
        copy.wait_recv()
        total = total + squares_in[k]
    mean_square = jnp.sum(total, axis=0, keepdims=True) / channels
    norm = jnp.broadcast_to(1.0 / jnp.sqrt(mean_square + 0.5), (128, rows)).T
    norm = jnp.concatenate([norm] * (TILE // 128), axis=1)

    for c in range(CHUNKS):

        def short(i, _, c=c):
            cols = pl.ds(pl.multiple_of(c * wide + i * TILE, TILE), TILE)
            x = stream[:, cols].astype(jnp.float32) * gain_ref[:, cols] * norm
            ext[c, own, pl.ds(pl.multiple_of(i * TILE, TILE), TILE)] = (
                sinner[:, cols].astype(jnp.float32) * x
            ).astype(jnp.bfloat16)
            return 0

        lax.fori_loop(0, tiles, short, 0)
        send_tail(c)

    for i, c in enumerate(others):
        landed(keys.at[c, own], key_sem.at[2 + i])
    send_key(0, late)
    for c in range(1, CHUNKS):
        send_key(c)

    lax.fori_loop(width // TILE // 2, width // TILE, spectra, 0)
    landed(blocks.at[pl.ds(3, 2)], load_sem.at[5])
    row = lax.broadcasted_iota(jnp.int32, (rows, 2 * rows), 0)
    column = lax.broadcasted_iota(jnp.int32, (rows, 2 * rows), 1)
    lower = (jnp.where(column >= rows, column - rows, column) <= row).astype(
        jnp.float32
    ).astype(jnp.bfloat16)

    def state_copy(c, target, member):
        return remote(
            group_state.at[c],
            states.at[c, group],
            e_send.at[target],
            e_recv.at[c, group],
            seq(target * GROUP + member),
        )

    def mix_chunk(c):
        @pl.when(has_prev)
        def _():
            t_copies[c].wait_recv()

        def mix(i, _):
            here = pl.ds(pl.multiple_of(i * TILE, TILE), TILE)
            cols = pl.ds(pl.multiple_of(c * wide + i * TILE, TILE), TILE)
            x = dot(fwd[...], ext[c, :, here])
            x_re, x_im = x[:rows], x[rows:]
            h_re, h_im = spectrum[:rows, cols], spectrum[rows:, cols]
            y = jnp.concatenate(
                [x_re * h_re - x_im * h_im, x_re * h_im + x_im * h_re], axis=0
            ).astype(jnp.bfloat16)
            conv = dot(inv[...], y)
            long_in = (
                linner[:, cols].astype(jnp.float32) * souter[:, cols].astype(jnp.float32) * conv
            ).astype(jnp.bfloat16)
            v = long_in.astype(jnp.float32) * inv_power[:, cols]
            high = v.astype(jnp.bfloat16)
            low = (v - high.astype(jnp.float32)).astype(jnp.bfloat16)
            sums = dot(lower, jnp.concatenate([high, low], axis=0))
            cum[:, cols] = sums
            own_state[c, :, here] = sums[rows - 1 :] * power[rows - 1 :, cols]
            return 0

        lax.fori_loop(0, tiles, mix, 0)

        @pl.when(jnp.logical_not(even))
        def _():
            remote(
                own_state.at[c], member_state.at[c], p_send.at[0], p_recv.at[c], seq(me - 1)
            ).start()

    def rate_of(c):
        return decay_ref[:, pl.ds(c * wide, wide)]

    def pair(c):
        @pl.when(first)
        def _():
            landed(member_state.at[c], p_recv.at[c])
            over = jnp.exp(-rate_of(c) * rows)
            pair_state[c] = own_state[c] * over + member_state[c]
            remote(
                pair_state.at[c], before_state.at[c], g_send.at[0], g_recv.at[c], seq(me + 2)
            ).start()

    def collect(c):
        @pl.when(borrows)
        def _():
            landed(member_state.at[c], p_recv.at[c])
            landed(before_state.at[c], g_recv.at[c])
            over = jnp.exp(-rate_of(c) * rows)
            group_state[c] = (before_state[c] * over + own_state[c]) * over + member_state[c]

            def send_state(target, _):
                state_copy(c, target, 0).start()
                state_copy(c, target, 2).start()
                return 0

            lax.fori_loop(group + 1, groups, send_state, 0)

    def spread(c):
        @pl.when(even)
        def _():
            over_group = jnp.exp(-rate_of(c) * (rows * GROUP))

            def arrive(j, state):
                landed(states.at[c, j], e_recv.at[c, j])
                return state * over_group + states[c, j]

            state = lax.fori_loop(0, group, arrive, jnp.zeros((1, wide), jnp.float32))
            over = jnp.exp(-rate_of(c) * rows)
            carry_in[c] = state

            @pl.when(borrows)
            def _():
                carry_in[c] = state * jnp.exp(-rate_of(c) * (2 * rows)) + before_state[c]

            next_state[c] = carry_in[c] * over + own_state[c]
            remote(
                next_state.at[c], carry_in.at[c], q_send.at[0], q_recv.at[c], seq(me + 1)
            ).start()

    def long_chunk(c):
        @pl.when(jnp.logical_not(even))
        def _():
            landed(carry_in.at[c], q_recv.at[c])

        rate = rate_of(c)
        carried = carry_in[c] * jnp.exp(-rate)
        z = 2.0 * rate
        scale = jnp.sqrt(jnp.tanh(0.5 * z) * (1.0 + jnp.exp(-z)))
        for i in range(tiles):
            here = pl.ds(i * TILE, TILE)
            cols = pl.ds(c * wide + i * TILE, TILE)
            part = slice(i * TILE, (i + 1) * TILE)
            conv = (cum[:, cols] + carried[:, part]) * power[:, cols]
            out = (
                louter[:, cols].astype(jnp.float32) * (conv * scale[:, part])
            ).astype(jnp.bfloat16)
            values[c, own, here] = out
            mixed[:, cols] = out

        direct = has_next
        if c == LENT:
            direct = jnp.logical_and(has_next, jnp.logical_not(lends))

            @pl.when(lends)
            def _():
                def lend_values(h, _):
                    here = pl.ds(pl.multiple_of(h * HEAD_DIM, HEAD_DIM), HEAD_DIM)
                    lent[:, here] = dot_tn(
                        lent_weights[h], values[LENT, own, here]
                    ).astype(jnp.bfloat16)
                    return 0

                lax.fori_loop(0, heads, lend_values, 0, unroll=8)
                lent_values.start()

        if c == 0:
            relay = jnp.logical_and(relays, group == 0)
            direct = jnp.logical_and(has_next, jnp.logical_not(relay))

            @pl.when(relay)
            def _():
                to_relay(values, c, CHUNKS + HALF, v_send).start()

        if c < HALF:
            direct = jnp.logical_and(direct, jnp.logical_not(jnp.logical_and(relays, later > 1)))

        @pl.when(direct)
        def _():
            v_copies[c].start()

    def lend_weights():
        @pl.when(lends)
        def _():
            lent_query.wait_recv()
            for h in range(heads):
                here = pl.ds(h * HEAD_DIM, HEAD_DIM)
                s = dot_nt(keys[LENT, own, here], next_query[:, here]) * HEAD_DIM ** (-0.5)
                top = jnp.max(s, axis=0, keepdims=True)
                e = jnp.exp(s - top)
                total = jnp.sum(e, axis=0, keepdims=True)
                lent_weights[h] = (e * (1.0 / total)).astype(jnp.bfloat16)
                stats[h : h + 1, :] = top
                stats[heads + h : heads + h + 1, :] = total
            lent_stats.start()

    valid = (column <= row + rows) & ((column >= rows) | has_prev)

    def score_chunk(c, when=True):
        if c == LENT:
            when = jnp.logical_not(borrows)

        @pl.when(jnp.logical_and(has_prev, when))
        def _():
            k_copies[c].wait_recv()

        def score(h, _):
            here = pl.ds(pl.multiple_of(h * HEAD_DIM, HEAD_DIM), HEAD_DIM)
            cols = pl.ds(pl.multiple_of(c * wide + h * HEAD_DIM, HEAD_DIM), HEAD_DIM)
            s = dot_nt(query[:, cols], keys[c, :, here]) * HEAD_DIM ** (-0.5)
            s = jnp.where(valid, s, -1e30)
            e = jnp.exp(s - jnp.max(s, axis=1, keepdims=True))
            e = e * (1.0 / jnp.sum(e, axis=1, keepdims=True))
            weights[c, h] = e.astype(jnp.bfloat16)
            return 0

        def run():
            lax.fori_loop(0, heads, score, 0, unroll=2)

        if when is True:
            run()
        else:
            pl.when(when)(run)

    def borrow():
        @pl.when(borrows)
        def _():
            upper = lax.broadcasted_iota(
                jnp.int32, (rows, rows), 0
            ) <= lax.broadcasted_iota(jnp.int32, (rows, rows), 1)
            for h in range(heads):
                here = pl.ds(h * HEAD_DIM, HEAD_DIM)
                cols = pl.ds(LENT * wide + h * HEAD_DIM, HEAD_DIM)
                s = dot_nt(keys[LENT, own, here], query[:, cols]) * HEAD_DIM ** (-0.5)
                s = jnp.where(upper, s, -1e30)
                top = jnp.max(s, axis=0, keepdims=True)
                e = jnp.exp(s - top)
                lent_weights[h] = e.astype(jnp.bfloat16)
                stats[h : h + 1, :] = top
                stats[heads + h : heads + h + 1, :] = jnp.sum(e, axis=0, keepdims=True)
            for h in range(heads):
                here = pl.ds(h * HEAD_DIM, HEAD_DIM)
                own_part[:, here] = dot_tn(lent_weights[h], values[LENT, own, here])

    def blend():
        @pl.when(borrows)
        def _():
            lent_stats.wait_recv()
            top, total = stats[:heads], stats[heads:]
            top_before, total_before = stats_in[:heads], stats_in[heads:]
            most = jnp.maximum(top, top_before)
            here_scale = jnp.exp(top - most)
            before_scale = jnp.exp(top_before - most) * total_before
            inverse = 1.0 / (total * here_scale + before_scale)
            both = jnp.concatenate([here_scale * inverse, before_scale * inverse], axis=0)
            both = jnp.concatenate(
                [both, jnp.zeros((HEAD_DIM - 2 * heads, rows), jnp.float32)], axis=0
            ).T
            for h in range(heads):
                here = pl.ds(h * HEAD_DIM, HEAD_DIM)
                own_part[:, here] = own_part[:, here] * both[:, h : h + 1]
                shares[:, here] = jnp.broadcast_to(
                    both[:, heads + h : heads + h + 1], (rows, HEAD_DIM)
                )

    def attend_chunk(c):
        @pl.when(has_prev)
        def _():
            v_copies[c].wait_recv()

        def gather(h, _):
            here = pl.ds(pl.multiple_of(h * HEAD_DIM, HEAD_DIM), HEAD_DIM)
            cols = pl.ds(pl.multiple_of(c * wide + h * HEAD_DIM, HEAD_DIM), HEAD_DIM)
            attended[:, cols] = dot(weights[c, h], values[c, :, here]).astype(jnp.bfloat16)
            return 0

        def finish():
            lax.fori_loop(0, heads, gather, 0, unroll=8)

        if c < LENT:
            finish()
            return
        pl.when(jnp.logical_not(borrows))(finish)

        @pl.when(borrows)
        def _():
            for i in range(tiles):
                here = pl.ds(i * TILE, TILE)
                cols = pl.ds(c * wide + i * TILE, TILE)
                attended[:, cols] = (
                    own_part[:, here]
                    + shares[:, here] * values[c, before, here].astype(jnp.float32)
                ).astype(jnp.bfloat16)

    mix_chunk(0)
    pair(0)
    pass_tail(2)
    mix_chunk(1)
    pair(1)
    collect(0)

    @pl.when(jnp.logical_and(borrows, origin))
    def _():
        lent_query.start()

    pass_tail(3)
    mix_chunk(2)
    pair(2)
    collect(1)
    landed(louter, load_sem.at[7])
    landed(query.at[:, rest], load_sem.at[8])
    spread(0)
    mix_chunk(3)
    pair(3)
    collect(2)
    spread(1)
    pass_key(0)
    long_chunk(0)
    long_chunk(1)
    pass_key(1)
    pass_key(2)
    score_chunk(0, jnp.logical_not(first))

    @pl.when(relays & (group > 0) & (later > 1))
    def _():
        v_copies[0].start()

    for c in range(1, HALF):

        @pl.when(jnp.logical_and(relays, later > 1))
        def _(c=c):
            v_copies[c].start()

    collect(3)
    spread(2)
    long_chunk(2)
    lend_weights()
    pass_key(3)
    score_chunk(1, jnp.logical_not(first))
    spread(3)
    long_chunk(3)
    pass_value()
    score_chunk(0, first)
    score_chunk(1, first)
    score_chunk(2)
    score_chunk(3)
    borrow()
    for c in range(CHUNKS - 1):
        attend_chunk(c)
    blend()
    attend_chunk(LENT)

    for copy in sq_copies:
        copy.wait_send()

    def sent(buffer, sem):
        pltpu.make_async_copy(buffer, buffer, sem).wait()

    @pl.when(jnp.logical_not(even))
    def _():
        sent(own_state, p_send.at[0])

    @pl.when(even)
    def _():
        sent(next_state, q_send.at[0])

    @pl.when(first)
    def _():
        sent(pair_state, g_send.at[0])

    @pl.when(borrows)
    def _():
        lent_query.wait_send()

        def all_sent(target, _):
            sent(states.at[:, pl.ds(0, 2)], e_send.at[target])
            return 0

        lax.fori_loop(group + 1, groups, all_sent, 0)

    for tails in (True, False):
        for fewer in (True, False):
            slots = pl.ds(HALF if fewer else 0, CHUNKS + tails * (HALF + 1) - fewer * HALF)

            @pl.when(forwards & (tail_relay == tails) & ((later == 1) == fewer))
            def _(slots=slots):
                sent(relayed.at[slots], r_send.at[0])

    @pl.when(lends)
    def _():
        sent(keys.at[pl.ds(0, LENT), own], k_send.at[0])
        lent_stats.wait_send()

    @pl.when(jnp.logical_and(has_next, jnp.logical_not(lends)))
    def _():
        sent(keys.at[:, own], k_send.at[0])

    @pl.when(has_next)
    def _():
        sent(ext.at[:, own], t_send.at[0])
        sent(values.at[:, own], v_send.at[0])


def store(mixed, attended, mixed_hbm, attended_hbm, sem):
    rows = mixed.shape[0]
    parts = [pl.ds(i * rows // STORES, rows // STORES) for i in range(STORES)]
    copies = [
        pltpu.make_async_copy(source.at[part], target.at[part], sem.at[k, i])
        for k, (source, target) in enumerate([(mixed, mixed_hbm), (attended, attended_hbm)])
        for i, part in enumerate(parts)
    ]
    for copy in copies:
        copy.start()
    for copy in copies:
        copy.wait()


def on_device(
    n,
    mp,
    stream,
    norm_gain,
    short_outer,
    short_inner,
    short_filter,
    long_outer,
    long_inner,
    long_decay,
    query_heads,
    key_heads,
):
    rows, width = stream.shape
    wide = width // CHUNKS
    heads = wide // HEAD_DIM
    groups = n // GROUP
    bf16, f32 = jnp.bfloat16, jnp.float32
    anywhere = pl.BlockSpec(memory_space=pltpu.HBM)
    vmem = pl.BlockSpec(memory_space=pltpu.VMEM)
    dma = pltpu.SemaphoreType.DMA

    def in_hbm(array):
        return pltpu.with_memory_space_constraint(array, pltpu.HBM)

    mixed, attended = pl.pallas_call(
        functools.partial(kernel, n, mp, float(width * mp)),
        out_shape=[jax.ShapeDtypeStruct((rows, width), bf16)] * 2,
        in_specs=[anywhere] * 11,
        out_specs=[vmem] * 2,
        scratch_shapes=[
            pltpu.VMEM((2, 1, width), f32),
            pltpu.VMEM((7, rows, width), bf16),
            pltpu.VMEM((3 * rows, 2 * rows), bf16),
        ]
        + [pltpu.VMEM((CHUNKS, 2 * rows, wide), bf16)] * 3
        + [pltpu.VMEM((CHUNKS + HALF + 1, rows, wide), bf16)]
        + [pltpu.VMEM((rows, wide), bf16)] * 2
        + [pltpu.VMEM((rows, wide), f32)] * 2
        + [pltpu.VMEM((rows, width), f32)] * 3
        + [
            pltpu.VMEM((2 * rows, width), f32),
            pltpu.VMEM((CHUNKS, heads, rows, 2 * rows), bf16),
            pltpu.VMEM((heads, rows, rows), bf16),
        ]
        + [pltpu.VMEM((2 * heads, rows), f32)] * 2
        + [
            pltpu.VMEM((8, rows), f32),
            pltpu.VMEM((mp - 1, 8, rows), f32),
        ]
        + [pltpu.VMEM((CHUNKS, 1, wide), f32)] * 7
        + [
            pltpu.VMEM((CHUNKS, groups, 1, wide), f32),
            dma((9,)),
            dma((CHUNKS,)),
            dma((mp - 1,)),
            dma((mp - 1,)),
        ]
        + [dma((1,)), dma((CHUNKS,))] * 3
        + [dma((1,)), dma((CHUNKS + HALF + 1,))]
        + [dma((1,)), dma((CHUNKS,))] * 3
        + [dma((groups,)), dma((CHUNKS, groups))]
        + [dma((2,))] * 2,
        compiler_params=pltpu.CompilerParams(
            collective_id=0, has_side_effects=True, vmem_limit_bytes=51 * 1024 * 1024
        ),
    )(
        in_hbm(norm_gain.reshape(1, width)),
        in_hbm(long_decay.reshape(1, width)),
        in_hbm(jnp.asarray(waves_of(rows), bf16)),
        stream,
        short_outer,
        short_inner,
        short_filter,
        long_outer,
        long_inner,
        query_heads,
        key_heads,
    )
    return pl.pallas_call(
        store,
        out_shape=[jax.ShapeDtypeStruct((rows, width), bf16)] * 2,
        in_specs=[vmem] * 2,
        out_specs=[anywhere] * 2,
        scratch_shapes=[dma((2, STORES))],
        compiler_params=pltpu.CompilerParams(vmem_limit_bytes=1024 * 1024),
    )(mixed, attended)


def solution(mesh):
    return jax.shard_map(
        functools.partial(on_device, mesh.shape["seq"], mesh.shape["mp"]),
        mesh=mesh,
        in_specs=(
            P("seq", "mp"),
            P("mp"),
            P("seq", "mp"),
            P("seq", "mp"),
            P(None, "mp"),
            P("seq", "mp"),
            P("seq", "mp"),
            P("mp"),
            P("seq", "mp"),
            P("seq", "mp"),
        ),
        out_specs=(P("seq", "mp"), P("seq", "mp")),
        check_vma=False,
    )
```

time: 42.2 us -> 39.5 us (0.936)
  Pallas kernels: 41 us -> 38.7 us
    pallas_call x1, Pallas kernels: 39.7 us -> 37.3 us  [on_device(): pl.pallas_call(functools.partial(kernel, n, mp, float(width * mp)), out_s...]
where the time goes in v2:
time: 39.5 us; the launch traced here: 39.3 us
  Pallas kernels  38.7 us (98%)
  between operations  0.64 us (2%)
    pallas_call x1, Pallas kernels, on_device(): pl.pallas_call(functools.partial(kernel, n, mp, float(width * mp)), out_s...  37.3 us
    pallas_call x1, Pallas kernels, on_device(): pl.pallas_call(store, out_shape=[jax.ShapeDtypeStruct((rows, width), bf16...  1.35 us

profile of v2, /device:TPU:24, one launch (start us, length us, event | category | flops | bytes accessed | tf_op | source)
XLA Modules:
  0.0 39.3 jit_solution(7598075313852775622)
XLA Ops:
  0.6 37.3 %shard_map.122 = (bf16[128,4096]{1,0:T(8,128)(2,1)S(1)}, bf16[128,4096]{1,0:T(8,128)(2,1)S(1)}) custom-call(f32[1,4096]{1,0:T(1,128)} %bitcast.2, f32[1,4096]{1,0:T(1,128)} %bitcast.3, bf16[384,256]{1,0:T(8,128)(2,1)} %constant.2.clone.waves_hbm, bf16[128,4096]{1,0:T(8,128)(2,1)} %stream_hbm.1, bf16[128,4096]{1,0:T(8,128)(2,1)} %souter_hbm.1, ...), custom_call_target="tpu_custom_call" | custom-call | tf_op jit(solution)/shard_map/pallas_call | solution.py:791
  38.0 1.3 %shard_map.123 = (bf16[128,4096]{1,0:T(8,128)(2,1)}, bf16[128,4096]{1,0:T(8,128)(2,1)}) custom-call(bf16[128,4096]{1,0:T(8,128)(2,1)S(1)} %get-tuple-element.4.mixed, bf16[128,4096]{1,0:T(8,128)(2,1)S(1)} %get-tuple-element.5.attended), custom_call_target="tpu_custom_call" | custom-call | tf_op jit(solution)/shard_map/pallas_call | solution.py:845

commit v3 on v2

--- a/solution.py
+++ b/solution.py
@@ -87,6 +87,7 @@
     before_state,
     group_state,
     next_state,
+    across_state,
     carry_in,
     states,
     load_sem,
@@ -99,14 +100,10 @@
     t_recv,
     v_send,
     v_recv,
-    r_send,
-    r_recv,
-    p_send,
-    p_recv,
-    q_send,
-    q_recv,
-    g_send,
-    g_recv,
+    cross_send,
+    cross_recv,
+    state_send,
+    state_recv,
     e_send,
     e_recv,
     lend_send,
@@ -152,7 +149,7 @@
     greet(me + 2, forwards)
     greet(me - 3, jnp.logical_and(first, group > 0))
 
-    @pl.when(even)
+    @pl.when(first)
     def _():
         def greet_earlier(j, _):
             pl.semaphore_signal(
@@ -163,7 +160,7 @@
         lax.fori_loop(0, group, greet_earlier, 0)
 
     greeted = has_next.astype(jnp.int32) + has_prev.astype(jnp.int32) + mp - 1
-    greeted += jnp.where(borrows, 2 * later, 0)
+    greeted += jnp.where(borrows, later, 0)
     greeted += (first | relays | forwards).astype(jnp.int32)
 
     for k in range(1, mp):
@@ -180,7 +177,6 @@
     def load_key(c, sem):
         load(key_hbm.at[:, pl.ds(c * wide, wide)], keys.at[c, own], sem)
 
-    others = [c for c in range(1, CHUNKS) if c != HALF]
     last = pl.ds(LENT * wide, wide)
     rest = pl.ds(0, LENT * wide)
     load(query_hbm.at[:, last], query.at[:, last], load_sem.at[6])
@@ -189,9 +185,6 @@
     load(stream_hbm, stream, load_sem.at[0])
     load(gain_hbm, gain_ref, load_sem.at[2])
     load(decay_hbm, decay_ref, load_sem.at[2])
-    load(waves_hbm, waves, load_sem.at[3])
-    load(filt_hbm, filt, load_sem.at[4])
-    load(sinner_hbm, sinner, load_sem.at[1])
 
     def remote(source, target, send, recv, device):
         return pltpu.make_async_remote_copy(
@@ -210,7 +203,7 @@
 
     def to_relay(buffer, c, slot, send):
         return remote(
-            buffer.at[c, own], relayed.at[slot], send.at[0], r_recv.at[slot], seq(me - 2)
+            buffer.at[c, own], relayed.at[slot], send.at[0], cross_recv.at[slot], seq(me - 2)
         )
 
     k_copies = [to_next(keys, c, k_send, k_recv) for c in range(CHUNKS)]
@@ -262,10 +255,10 @@
         @pl.when(jnp.logical_and(forwards, when))
         def _():
             remote(
-                buffer.at[c, own], relayed.at[slot], k_send.at[0], r_recv.at[slot], seq(me + 2)
+                buffer.at[c, own], relayed.at[slot], k_send.at[0], cross_recv.at[slot], seq(me + 2)
             ).wait_recv()
             remote(
-                relayed.at[slot], buffer.at[c, before], r_send.at[0], recv.at[c], seq(me + 3)
+                relayed.at[slot], buffer.at[c, before], cross_send.at[0], recv.at[c], seq(me + 3)
             ).start()
 
     def pass_key(c):
@@ -295,13 +288,19 @@
 
     landed(keys.at[0, own], key_sem.at[0])
     send_key(0, jnp.logical_not(late))
+    ahead = jnp.logical_and(relays, later == 1)
     landed(keys.at[HALF, own], key_sem.at[1])
-    for c in others:
-        load_key(c, key_sem.at[2 + others.index(c)])
+    send_key(HALF, ahead)
+    load(waves_hbm, waves, load_sem.at[3])
+    load(filt_hbm, filt, load_sem.at[4])
+    load(sinner_hbm, sinner, load_sem.at[1])
+    others = [c for c in range(1, CHUNKS) if c != HALF]
+    for i, c in enumerate(others):
+        load_key(c, key_sem.at[2 + i])
     load(souter_hbm, souter, load_sem.at[5])
     load(linner_hbm, linner, load_sem.at[5])
-    load(louter_hbm, louter, load_sem.at[7])
-    load(query_hbm.at[:, rest], query.at[:, rest], load_sem.at[8])
+    load(louter_hbm, louter, load_sem.at[5])
+    load(query_hbm.at[:, rest], query.at[:, rest], load_sem.at[7])
     landed(stream, load_sem.at[0])
 
     def square(i, acc):
@@ -372,23 +371,23 @@
         landed(keys.at[c, own], key_sem.at[2 + i])
     send_key(0, late)
     for c in range(1, CHUNKS):
-        send_key(c)
+        send_key(c, jnp.logical_not(ahead) if c == HALF else True)
 
     lax.fori_loop(width // TILE // 2, width // TILE, spectra, 0)
-    landed(blocks.at[pl.ds(3, 2)], load_sem.at[5])
+    landed(blocks.at[pl.ds(3, 3)], load_sem.at[5])
     row = lax.broadcasted_iota(jnp.int32, (rows, 2 * rows), 0)
     column = lax.broadcasted_iota(jnp.int32, (rows, 2 * rows), 1)
     lower = (jnp.where(column >= rows, column - rows, column) <= row).astype(
         jnp.float32
     ).astype(jnp.bfloat16)
 
-    def state_copy(c, target, member):
+    def state_copy(c, target):
         return remote(
             group_state.at[c],
             states.at[c, group],
             e_send.at[target],
-            e_recv.at[c, group],
-            seq(target * GROUP + member),
+            e_recv.at[c],
+            seq(target * GROUP),
         )
 
     def mix_chunk(c):
@@ -422,7 +421,7 @@
         @pl.when(jnp.logical_not(even))
         def _():
             remote(
-                own_state.at[c], member_state.at[c], p_send.at[0], p_recv.at[c], seq(me - 1)
+                own_state.at[c], member_state.at[c], state_send.at[0], state_recv.at[c], seq(me - 1)
             ).start()
 
     def rate_of(c):
@@ -431,54 +430,67 @@
     def pair(c):
         @pl.when(first)
         def _():
-            landed(member_state.at[c], p_recv.at[c])
+            landed(member_state.at[c], state_recv.at[c])
             over = jnp.exp(-rate_of(c) * rows)
             pair_state[c] = own_state[c] * over + member_state[c]
             remote(
-                pair_state.at[c], before_state.at[c], g_send.at[0], g_recv.at[c], seq(me + 2)
+                pair_state.at[c], before_state.at[c], cross_send.at[0], cross_recv.at[c], seq(me + 2)
             ).start()
 
     def collect(c):
         @pl.when(borrows)
         def _():
-            landed(member_state.at[c], p_recv.at[c])
-            landed(before_state.at[c], g_recv.at[c])
+            landed(member_state.at[c], state_recv.at[c])
+            landed(before_state.at[c], cross_recv.at[c])
             over = jnp.exp(-rate_of(c) * rows)
             group_state[c] = (before_state[c] * over + own_state[c]) * over + member_state[c]
 
             def send_state(target, _):
-                state_copy(c, target, 0).start()
-                state_copy(c, target, 2).start()
+                state_copy(c, target).start()
                 return 0
 
             lax.fori_loop(group + 1, groups, send_state, 0)
 
     def spread(c):
-        @pl.when(even)
-        def _():
+        @pl.when(first)
+        def _():
+            for g in range(1, groups):
+
+                @pl.when(group == g)
+                def _(g=g):
+                    landed(states.at[c, pl.ds(0, g)], e_recv.at[c])
+
             over_group = jnp.exp(-rate_of(c) * (rows * GROUP))
 
             def arrive(j, state):
-                landed(states.at[c, j], e_recv.at[c, j])
                 return state * over_group + states[c, j]
 
             state = lax.fori_loop(0, group, arrive, jnp.zeros((1, wide), jnp.float32))
             over = jnp.exp(-rate_of(c) * rows)
             carry_in[c] = state
-
-            @pl.when(borrows)
-            def _():
-                carry_in[c] = state * jnp.exp(-rate_of(c) * (2 * rows)) + before_state[c]
-
-            next_state[c] = carry_in[c] * over + own_state[c]
+            next_state[c] = state * over + own_state[c]
+            give_next(c)
+            across_state[c] = state * jnp.exp(-rate_of(c) * (2 * rows)) + pair_state[c]
             remote(
-                next_state.at[c], carry_in.at[c], q_send.at[0], q_recv.at[c], seq(me + 1)
+                across_state.at[c], carry_in.at[c], cross_send.at[1], e_recv.at[c], seq(me + 2)
             ).start()
+
+    def give_next(c):
+        remote(
+            next_state.at[c], carry_in.at[c], state_send.at[0], state_recv.at[c], seq(me + 1)
+        ).start()
+
+    def hand_on(c):
+        @pl.when(borrows)
+        def _():
+            landed(carry_in.at[c], e_recv.at[c])
+            next_state[c] = carry_in[c] * jnp.exp(-rate_of(c) * rows) + own_state[c]
+            give_next(c)
 
     def long_chunk(c):
         @pl.when(jnp.logical_not(even))
         def _():
-            landed(carry_in.at[c], q_recv.at[c])
+            landed(carry_in.at[c], state_recv.at[c])
 
         rate = rate_of(c)
         carried = carry_in[c] * jnp.exp(-rate)
@@ -519,8 +531,8 @@
             def _():
                 to_relay(values, c, CHUNKS + HALF, v_send).start()
 
-        if c < HALF:
-            direct = jnp.logical_and(direct, jnp.logical_not(jnp.logical_and(relays, later > 1)))
+        if c == 0:
+            direct = jnp.logical_and(direct, jnp.logical_not(held))
 
         @pl.when(direct)
         def _():
@@ -543,11 +555,11 @@
 
     valid = (column <= row + rows) & ((column >= rows) | has_prev)
 
-    def score_chunk(c, when=True):
+    def score_chunk(c, when=True, half=None):
         if c == LENT:
             when = jnp.logical_not(borrows)
 
-        @pl.when(jnp.logical_and(has_prev, when))
+        @pl.when(jnp.logical_and(has_prev, when if half != 1 else False))
         def _():
             k_copies[c].wait_recv()
 
@@ -561,8 +573,11 @@
             weights[c, h] = e.astype(jnp.bfloat16)
             return 0
 
+        start = heads // 2 if half == 1 else 0
+        stop = heads // 2 if half == 0 else heads
+
         def run():
-            lax.fori_loop(0, heads, score, 0, unroll=2)
+            lax.fori_loop(start, stop, score, 0, unroll=2)
 
         if when is True:
             run()
@@ -654,37 +669,36 @@
     mix_chunk(2)
     pair(2)
     collect(1)
-    landed(louter, load_sem.at[7])
-    landed(query.at[:, rest], load_sem.at[8])
+    landed(query.at[:, rest], load_sem.at[7])
     spread(0)
     mix_chunk(3)
     pair(3)
     collect(2)
     spread(1)
     pass_key(0)
+    hand_on(0)
+    held = relays & (group > 0)
     long_chunk(0)
+    score_chunk(0, jnp.logical_not(first), 0)
+
+    @pl.when(held)
+    def _():
+        v_copies[0].start()
+
+    score_chunk(0, jnp.logical_not(first), 1)
+    collect(3)
+    spread(2)
+    hand_on(1)
     long_chunk(1)
     pass_key(1)
     pass_key(2)
-    score_chunk(0, jnp.logical_not(first))
-
-    @pl.when(relays & (group > 0) & (later > 1))
-    def _():
-        v_copies[0].start()
-
-    for c in range(1, HALF):
-
-        @pl.when(jnp.logical_and(relays, later > 1))
-        def _(c=c):
-            v_copies[c].start()
-
-    collect(3)
-    spread(2)
+    hand_on(2)
     long_chunk(2)
     lend_weights()
     pass_key(3)
     score_chunk(1, jnp.logical_not(first))
     spread(3)
+    hand_on(3)
     long_chunk(3)
     pass_value()
     score_chunk(0, first)
@@ -705,22 +719,23 @@
 
     @pl.when(jnp.logical_not(even))
     def _():
-        sent(own_state, p_send.at[0])
+        sent(own_state, state_send.at[0])
 
     @pl.when(even)
     def _():
-        sent(next_state, q_send.at[0])
+        sent(next_state, state_send.at[0])
 
     @pl.when(first)
     def _():
-        sent(pair_state, g_send.at[0])
+        sent(pair_state, cross_send.at[0])
+        sent(across_state, cross_send.at[1])
 
     @pl.when(borrows)
     def _():
         lent_query.wait_send()
 
         def all_sent(target, _):
-            sent(states.at[:, pl.ds(0, 2)], e_send.at[target])
+            sent(group_state, e_send.at[target])
             return 0
 
         lax.fori_loop(group + 1, groups, all_sent, 0)
@@ -731,7 +746,7 @@
 
             @pl.when(forwards & (tail_relay == tails) & ((later == 1) == fewer))
             def _(slots=slots):
-                sent(relayed.at[slots], r_send.at[0])
+                sent(relayed.at[slots], cross_send.at[0])
 
     @pl.when(lends)
     def _():
@@ -813,18 +828,18 @@
             pltpu.VMEM((8, rows), f32),
             pltpu.VMEM((mp - 1, 8, rows), f32),
         ]
-        + [pltpu.VMEM((CHUNKS, 1, wide), f32)] * 7
+        + [pltpu.VMEM((CHUNKS, 1, wide), f32)] * 8
         + [
             pltpu.VMEM((CHUNKS, groups, 1, wide), f32),
-            dma((9,)),
+            dma((8,)),
             dma((CHUNKS,)),
             dma((mp - 1,)),
             dma((mp - 1,)),
         ]
         + [dma((1,)), dma((CHUNKS,))] * 3
-        + [dma((1,)), dma((CHUNKS + HALF + 1,))]
-        + [dma((1,)), dma((CHUNKS,))] * 3
-        + [dma((groups,)), dma((CHUNKS, groups))]
+        + [dma((2,)), dma((CHUNKS + HALF + 1,))]
+        + [dma((1,)), dma((CHUNKS,))]
+        + [dma((groups,)), dma((CHUNKS,))]
         + [dma((2,))] * 2,
         compiler_params=pltpu.CompilerParams(
             collective_id=0, has_side_effects=True, vmem_limit_bytes=51 * 1024 * 1024

time: 39.5 us -> 38.7 us (0.980)
  Pallas kernels: 38.7 us -> 37.9 us
    pallas_call x1, Pallas kernels: 37.3 us -> 36.6 us  [on_device(): pl.pallas_call(functools.partial(kernel, n, mp, float(width * mp)), out_s...]
where the time goes in v3:
time: 38.7 us; the launch traced here: 38.6 us
  Pallas kernels  37.9 us (98%)
  between operations  0.64 us (2%)
    pallas_call x1, Pallas kernels, on_device(): pl.pallas_call(functools.partial(kernel, n, mp, float(width * mp)), out_s...  36.6 us
    pallas_call x1, Pallas kernels, on_device(): pl.pallas_call(store, out_shape=[jax.ShapeDtypeStruct((rows, width), bf16...  1.35 us

profile of v3, /device:TPU:24, one launch (start us, length us, event | category | flops | bytes accessed | tf_op | source)
XLA Modules:
  0.0 38.6 jit_solution(10265673773247715907)
XLA Ops:
  0.6 36.6 %shard_map.122 = (bf16[128,4096]{1,0:T(8,128)(2,1)S(1)}, bf16[128,4096]{1,0:T(8,128)(2,1)S(1)}) custom-call(f32[1,4096]{1,0:T(1,128)} %bitcast.2, f32[1,4096]{1,0:T(1,128)} %bitcast.3, bf16[384,256]{1,0:T(8,128)(2,1)} %constant.2.clone.waves_hbm, bf16[128,4096]{1,0:T(8,128)(2,1)} %stream_hbm.1, bf16[128,4096]{1,0:T(8,128)(2,1)} %souter_hbm.1, ...), custom_call_target="tpu_custom_call" | custom-call | tf_op jit(solution)/shard_map/pallas_call | solution.py:806
  37.2 1.3 %shard_map.123 = (bf16[128,4096]{1,0:T(8,128)(2,1)}, bf16[128,4096]{1,0:T(8,128)(2,1)}) custom-call(bf16[128,4096]{1,0:T(8,128)(2,1)S(1)} %get-tuple-element.4.mixed, bf16[128,4096]{1,0:T(8,128)(2,1)S(1)} %get-tuple-element.5.attended), custom_call_target="tpu_custom_call" | custom-call | tf_op jit(solution)/shard_map/pallas_call | solution.py:860

commit v4 on v3

--- a/solution.py
+++ b/solution.py
@@ -12,6 +12,7 @@
 CHUNKS = 4
 HALF = CHUNKS // 2
 LENT = CHUNKS - 1
+KEPT = 2
 GROUP = 4
 TILE = 256
 STORES = 2
@@ -118,6 +119,7 @@
     wide = width // CHUNKS
     tiles = wide // TILE
     heads = wide // HEAD_DIM
+    keep = KEPT * HEAD_DIM
     has_next = me < n - 1
     has_prev = me > 0
     groups = n // GROUP
@@ -177,8 +179,8 @@
     def load_key(c, sem):
         load(key_hbm.at[:, pl.ds(c * wide, wide)], keys.at[c, own], sem)
 
-    last = pl.ds(LENT * wide, wide)
-    rest = pl.ds(0, LENT * wide)
+    last = pl.ds(LENT * wide + keep, wide - keep)
+    rest = pl.ds(0, LENT * wide + keep)
     load(query_hbm.at[:, last], query.at[:, last], load_sem.at[6])
     load_key(0, key_sem.at[0])
     load_key(HALF, key_sem.at[1])
@@ -214,8 +216,25 @@
     )
     lent_stats = remote(stats, stats_in, lend_send.at[1], lend_recv.at[1], seq(me + 1))
     lent_values = remote(
-        lent, values.at[LENT, before], v_send.at[0], v_recv.at[LENT], seq(me + 1)
+        lent,
+        values.at[LENT, before, pl.ds(keep, wide - keep)],
+        lend_send.at[4],
+        v_recv.at[CHUNKS],
+        seq(me + 1),
     )
+
+    def kept(buffer, send, recv):
+        part = pl.ds(0, keep)
+        return remote(
+            buffer.at[LENT, own, part],
+            buffer.at[LENT, before, part],
+            send,
+            recv.at[LENT],
+            seq(me + 1),
+        )
+
+    kept_keys = kept(keys, lend_send.at[2], k_recv)
+    kept_values = kept(values, lend_send.at[3], v_recv)
 
     key_relay = [
         later > 1 if c >= HALF else True for c in range(CHUNKS)
@@ -228,6 +247,10 @@
         direct = jnp.logical_and(has_next, jnp.logical_not(relay))
         if c == LENT:
             direct = jnp.logical_and(direct, jnp.logical_not(lends))
+
+            @pl.when(lends)
+            def _():
+                kept_keys.start()
 
         @pl.when(jnp.logical_and(relay, when))
         def _():
@@ -513,14 +536,17 @@
 
             @pl.when(lends)
             def _():
+                kept_values.start()
+
                 def lend_values(h, _):
                     here = pl.ds(pl.multiple_of(h * HEAD_DIM, HEAD_DIM), HEAD_DIM)
+                    there = pl.ds(pl.multiple_of(keep + h * HEAD_DIM, HEAD_DIM), HEAD_DIM)
                     lent[:, here] = dot_tn(
-                        lent_weights[h], values[LENT, own, here]
+                        lent_weights[h], values[LENT, own, there]
                     ).astype(jnp.bfloat16)
                     return 0
 
-                lax.fori_loop(0, heads, lend_values, 0, unroll=8)
+                lax.fori_loop(0, heads - KEPT, lend_values, 0, unroll=heads - KEPT)
                 lent_values.start()
 
         if c == 0:
@@ -542,9 +568,11 @@
         @pl.when(lends)
         def _():
             lent_query.wait_recv()
-            for h in range(heads):
+            stats[...] = jnp.ones(stats.shape, stats.dtype)
+            for h in range(heads - KEPT):
                 here = pl.ds(h * HEAD_DIM, HEAD_DIM)
-                s = dot_nt(keys[LENT, own, here], next_query[:, here]) * HEAD_DIM ** (-0.5)
+                there = pl.ds(keep + h * HEAD_DIM, HEAD_DIM)
+                s = dot_nt(keys[LENT, own, there], next_query[:, here]) * HEAD_DIM ** (-0.5)
                 top = jnp.max(s, axis=0, keepdims=True)
                 e = jnp.exp(s - top)
                 total = jnp.sum(e, axis=0, keepdims=True)
@@ -558,6 +586,10 @@
     def score_chunk(c, when=True, half=None):
         if c == LENT:
             when = jnp.logical_not(borrows)
+
+            @pl.when(borrows)
+            def _():
+                kept_keys.wait_recv()
 
         @pl.when(jnp.logical_and(has_prev, when if half != 1 else False))
         def _():
@@ -573,8 +605,8 @@
             weights[c, h] = e.astype(jnp.bfloat16)
             return 0
 
-        start = heads // 2 if half == 1 else 0
-        stop = heads // 2 if half == 0 else heads
+        start = 2 if half == 1 else 0
+        stop = 2 if half == 0 else heads
 
         def run():
             lax.fori_loop(start, stop, score, 0, unroll=2)
@@ -583,6 +615,11 @@
             run()
         else:
             pl.when(when)(run)
+        if c == LENT:
+
+            @pl.when(borrows)
+            def _():
+                lax.fori_loop(0, KEPT, score, 0, unroll=2)
 
     def borrow():
         @pl.when(borrows)
@@ -590,9 +627,10 @@
             upper = lax.broadcasted_iota(
                 jnp.int32, (rows, rows), 0
             ) <= lax.broadcasted_iota(jnp.int32, (rows, rows), 1)
-            for h in range(heads):
-                here = pl.ds(h * HEAD_DIM, HEAD_DIM)
-                cols = pl.ds(LENT * wide + h * HEAD_DIM, HEAD_DIM)
+            stats[...] = jnp.ones(stats.shape, stats.dtype)
+            for h in range(heads - KEPT):
+                here = pl.ds(keep + h * HEAD_DIM, HEAD_DIM)
+                cols = pl.ds(LENT * wide + keep + h * HEAD_DIM, HEAD_DIM)
                 s = dot_nt(keys[LENT, own, here], query[:, cols]) * HEAD_DIM ** (-0.5)
                 s = jnp.where(upper, s, -1e30)
                 top = jnp.max(s, axis=0, keepdims=True)
@@ -600,8 +638,8 @@
                 lent_weights[h] = e.astype(jnp.bfloat16)
                 stats[h : h + 1, :] = top
                 stats[heads + h : heads + h + 1, :] = jnp.sum(e, axis=0, keepdims=True)
-            for h in range(heads):
-                here = pl.ds(h * HEAD_DIM, HEAD_DIM)
+            for h in range(heads - KEPT):
+                here = pl.ds(keep + h * HEAD_DIM, HEAD_DIM)
                 own_part[:, here] = dot_tn(lent_weights[h], values[LENT, own, here])
 
     def blend():
@@ -618,15 +656,19 @@
             both = jnp.concatenate(
                 [both, jnp.zeros((HEAD_DIM - 2 * heads, rows), jnp.float32)], axis=0
             ).T
-            for h in range(heads):
-                here = pl.ds(h * HEAD_DIM, HEAD_DIM)
+            for h in range(heads - KEPT):
+                here = pl.ds(keep + h * HEAD_DIM, HEAD_DIM)
                 own_part[:, here] = own_part[:, here] * both[:, h : h + 1]
                 shares[:, here] = jnp.broadcast_to(
                     both[:, heads + h : heads + h + 1], (rows, HEAD_DIM)
                 )
 
     def attend_chunk(c):
-        @pl.when(has_prev)
+        when = has_prev
+        if c == LENT:
+            when = jnp.logical_and(has_prev, jnp.logical_not(borrows))
+
+        @pl.when(when)
         def _():
             v_copies[c].wait_recv()
 
@@ -646,7 +688,10 @@
 
         @pl.when(borrows)
         def _():
-            for i in range(tiles):
+            kept_values.wait_recv()
+            lax.fori_loop(0, KEPT, gather, 0, unroll=KEPT)
+            lent_values.wait_recv()
+            for i in range(keep // TILE, tiles):
                 here = pl.ds(i * TILE, TILE)
                 cols = pl.ds(c * wide + i * TILE, TILE)
                 attended[:, cols] = (
@@ -751,14 +796,16 @@
     @pl.when(lends)
     def _():
         sent(keys.at[pl.ds(0, LENT), own], k_send.at[0])
+        sent(ext.at[:, own], t_send.at[0])
+        sent(values.at[pl.ds(0, LENT), own], v_send.at[0])
         lent_stats.wait_send()
+        kept_keys.wait_send()
+        kept_values.wait_send()
+        lent_values.wait_send()
 
     @pl.when(jnp.logical_and(has_next, jnp.logical_not(lends)))
     def _():
         sent(keys.at[:, own], k_send.at[0])
-
-    @pl.when(has_next)
-    def _():
         sent(ext.at[:, own], t_send.at[0])
         sent(values.at[:, own], v_send.at[0])
 
@@ -815,7 +862,7 @@
         ]
         + [pltpu.VMEM((CHUNKS, 2 * rows, wide), bf16)] * 3
         + [pltpu.VMEM((CHUNKS + HALF + 1, rows, wide), bf16)]
-        + [pltpu.VMEM((rows, wide), bf16)] * 2
+        + [pltpu.VMEM((rows, wide - KEPT * HEAD_DIM), bf16)] * 2
         + [pltpu.VMEM((rows, wide), f32)] * 2
         + [pltpu.VMEM((rows, width), f32)] * 3
         + [
@@ -836,11 +883,12 @@
             dma((mp - 1,)),
             dma((mp - 1,)),
         ]
-        + [dma((1,)), dma((CHUNKS,))] * 3
+        + [dma((1,)), dma((CHUNKS,))] * 2
+        + [dma((1,)), dma((CHUNKS + 1,))]
         + [dma((2,)), dma((CHUNKS + HALF + 1,))]
         + [dma((1,)), dma((CHUNKS,))]
         + [dma((groups,)), dma((CHUNKS,))]
-        + [dma((2,))] * 2,
+        + [dma((5,)), dma((2,))],
         compiler_params=pltpu.CompilerParams(
             collective_id=0, has_side_effects=True, vmem_limit_bytes=51 * 1024 * 1024
         ),

time: 38.7 us -> 38.4 us (level)
  no operation moved by 1% of the time
where the time goes in v4:
time: 38.4 us; the launch traced here: 38.3 us
  Pallas kernels  37.6 us (98%)
  between operations  0.64 us (2%)
    pallas_call x1, Pallas kernels, on_device(): pl.pallas_call(functools.partial(kernel, n, mp, float(width * mp)), out_s...  36.3 us
    pallas_call x1, Pallas kernels, on_device(): pl.pallas_call(store, out_shape=[jax.ShapeDtypeStruct((rows, width), bf16...  1.35 us

profile of v4, /device:TPU:24, one launch (start us, length us, event | category | flops | bytes accessed | tf_op | source)
XLA Modules:
  0.0 38.3 jit_solution(12815723799942565819)
XLA Ops:
  0.6 36.3 %shard_map.122 = (bf16[128,4096]{1,0:T(8,128)(2,1)S(1)}, bf16[128,4096]{1,0:T(8,128)(2,1)S(1)}) custom-call(f32[1,4096]{1,0:T(1,128)} %bitcast.2, f32[1,4096]{1,0:T(1,128)} %bitcast.3, bf16[384,256]{1,0:T(8,128)(2,1)} %constant.2.clone.waves_hbm, bf16[128,4096]{1,0:T(8,128)(2,1)} %stream_hbm.1, bf16[128,4096]{1,0:T(8,128)(2,1)} %souter_hbm.1, ...), custom_call_target="tpu_custom_call" | custom-call | tf_op jit(solution)/shard_map/pallas_call | solution.py:853
  36.9 1.3 %shard_map.123 = (bf16[128,4096]{1,0:T(8,128)(2,1)}, bf16[128,4096]{1,0:T(8,128)(2,1)}) custom-call(bf16[128,4096]{1,0:T(8,128)(2,1)S(1)} %get-tuple-element.4.mixed, bf16[128,4096]{1,0:T(8,128)(2,1)S(1)} %get-tuple-element.5.attended), custom_call_target="tpu_custom_call" | custom-call | tf_op jit(solution)/shard_map/pallas_call | solution.py:908

commit v5 on v4

--- a/solution.py
+++ b/solution.py
@@ -300,6 +300,19 @@
             values[c, :rows, :] = jnp.zeros((rows, wide), values.dtype)
             ext[c, :rows, :] = jnp.zeros((rows, wide), ext.dtype)
 
+    def sum_squares():
+        landed(stream, load_sem.at[0])
+
+        def square(i, acc):
+            x = stream[:, pl.ds(pl.multiple_of(i * 128, 128), 128)].astype(jnp.float32)
+            return acc + x * x
+
+        total = lax.fori_loop(
+            0, width // 128, square, jnp.zeros((rows, 128), jnp.float32), unroll=4
+        )
+        squares[...] = jnp.sum(total.T.reshape(128 // 8, 8, rows), axis=0)
+
+    pl.when(jnp.logical_not(even))(sum_squares)
     pl.semaphore_wait(barrier, greeted)
     origin = group == 0
     late = jnp.logical_and(relays, origin)
@@ -324,16 +337,7 @@
     load(linner_hbm, linner, load_sem.at[5])
     load(louter_hbm, louter, load_sem.at[5])
     load(query_hbm.at[:, rest], query.at[:, rest], load_sem.at[7])
-    landed(stream, load_sem.at[0])
-
-    def square(i, acc):
-        x = stream[:, pl.ds(pl.multiple_of(i * 128, 128), 128)].astype(jnp.float32)
-        return acc + x * x
-
-    total = lax.fori_loop(
-        0, width // 128, square, jnp.zeros((rows, 128), jnp.float32), unroll=4
-    )
-    squares[...] = jnp.sum(total.T.reshape(128 // 8, 8, rows), axis=0)
+    pl.when(even)(sum_squares)
     sq_copies = [
         pltpu.make_async_remote_copy(
             src_ref=squares,

time: 38.4 us -> 38.3 us (level)
  no operation moved by 1% of the time
where the time goes in v5:
time: 38.3 us; the launch traced here: 38.1 us
  Pallas kernels  37.5 us (98%)
  between operations  0.64 us (2%)
    pallas_call x1, Pallas kernels, on_device(): pl.pallas_call(functools.partial(kernel, n, mp, float(width * mp)), out_s...  36.1 us
    pallas_call x1, Pallas kernels, on_device(): pl.pallas_call(store, out_shape=[jax.ShapeDtypeStruct((rows, width), bf16...  1.35 us

profile of v5, /device:TPU:24, one launch (start us, length us, event | category | flops | bytes accessed | tf_op | source)
XLA Modules:
  0.0 38.1 jit_solution(13623837807566071470)
XLA Ops:
  0.6 36.1 %shard_map.122 = (bf16[128,4096]{1,0:T(8,128)(2,1)S(1)}, bf16[128,4096]{1,0:T(8,128)(2,1)S(1)}) custom-call(f32[1,4096]{1,0:T(1,128)} %bitcast.2, f32[1,4096]{1,0:T(1,128)} %bitcast.3, bf16[384,256]{1,0:T(8,128)(2,1)} %constant.2.clone.waves_hbm, bf16[128,4096]{1,0:T(8,128)(2,1)} %stream_hbm.1, bf16[128,4096]{1,0:T(8,128)(2,1)} %souter_hbm.1, ...), custom_call_target="tpu_custom_call" | custom-call | tf_op jit(solution)/shard_map/pallas_call | solution.py:857
  36.8 1.3 %shard_map.123 = (bf16[128,4096]{1,0:T(8,128)(2,1)}, bf16[128,4096]{1,0:T(8,128)(2,1)}) custom-call(bf16[128,4096]{1,0:T(8,128)(2,1)S(1)} %get-tuple-element.4.mixed, bf16[128,4096]{1,0:T(8,128)(2,1)S(1)} %get-tuple-element.5.attended), custom_call_target="tpu_custom_call" | custom-call | tf_op jit(solution)/shard_map/pallas_call | solution.py:912

commit v6 on v5

--- a/solution.py
+++ b/solution.py
@@ -726,7 +726,7 @@
     spread(1)
     pass_key(0)
     hand_on(0)
-    held = relays & (group > 0)
+    held = relays & (group > 0) & (later > 1)
     long_chunk(0)
     score_chunk(0, jnp.logical_not(first), 0)
 

time: 38.3 us -> 38.2 us (level)
  Pallas kernels: 37.5 us -> 37.1 us
where the time goes in v6:
time: 38.2 us; the launch traced here: 37.7 us
  Pallas kernels  37.1 us (97%)
  between operations  0.64 us (2%)
    pallas_call x1, Pallas kernels, on_device(): pl.pallas_call(functools.partial(kernel, n, mp, float(width * mp)), out_s...  35.8 us
    pallas_call x1, Pallas kernels, on_device(): pl.pallas_call(store, out_shape=[jax.ShapeDtypeStruct((rows, width), bf16...  1.35 us

profile of v6, /device:TPU:24, one launch (start us, length us, event | category | flops | bytes accessed | tf_op | source)
XLA Modules:
  0.0 37.7 jit_solution(10075215746691447557)
XLA Ops:
  0.6 35.8 %shard_map.122 = (bf16[128,4096]{1,0:T(8,128)(2,1)S(1)}, bf16[128,4096]{1,0:T(8,128)(2,1)S(1)}) custom-call(f32[1,4096]{1,0:T(1,128)} %bitcast.2, f32[1,4096]{1,0:T(1,128)} %bitcast.3, bf16[384,256]{1,0:T(8,128)(2,1)} %constant.2.clone.waves_hbm, bf16[128,4096]{1,0:T(8,128)(2,1)} %stream_hbm.1, bf16[128,4096]{1,0:T(8,128)(2,1)} %souter_hbm.1, ...), custom_call_target="tpu_custom_call" | custom-call | tf_op jit(solution)/shard_map/pallas_call | solution.py:857
  36.4 1.3 %shard_map.123 = (bf16[128,4096]{1,0:T(8,128)(2,1)}, bf16[128,4096]{1,0:T(8,128)(2,1)}) custom-call(bf16[128,4096]{1,0:T(8,128)(2,1)S(1)} %get-tuple-element.4.mixed, bf16[128,4096]{1,0:T(8,128)(2,1)S(1)} %get-tuple-element.5.attended), custom_call_target="tpu_custom_call" | custom-call | tf_op jit(solution)/shard_map/pallas_call | solution.py:912
